TPU v7x, 128 devices: a whole 4x4x4 slice. The times are simulated.
128 devices in a mesh: gen: 4 (over x_lo, core), bank: 32 (over z, y, x_hi).
Axes of the slice: x: 4 (x_hi: 2, x_lo: 2; x = x_hi * 2 + x_lo), y: 4, z: 4, core: 2. Of those that a mesh axis runs over, the one named last changes fastest.
Arguments:
- latents: bfloat16 [8192, 4096], P(('gen', 'bank')), may hold values from -6 to 6
- shift: bfloat16 [8192, 4096], P(('gen', 'bank')), may hold values from -3 to 3
- scale_mod: bfloat16 [8192, 4096], P(('gen', 'bank')), may hold values from -3 to 3
- head_weight: bfloat16 [4096, 1024], P('gen'), may hold values from -0.09375 to 0.09375
- bank: bfloat16 [65536, 1024], P('bank'), may hold values from -8 to 8
Outputs:
- update: float32 [4096, 1024], P(('gen', 'bank'))
All inputs are finite; a program needn't handle non-finite values.
Results may differ from a plain program's by a relative error of at most 0.0042.
Values may be sent and summed in bfloat16 or wider, within the bound.
A program may use at most 128 MiB of HBM per device.

v0:
```python
import functools

import jax
import jax.numpy as jnp
from jax import lax
from jax.sharding import Mesh
from jax.sharding import PartitionSpec as P

GEN = ("gen_0", "gen_1")
BANK = ("bank_0", "bank_1", "bank_2")
GEN_BANK = ("gen_0", "gen_1", "bank_0", "bank_1", "bank_2")


kernel_scale = 32.0


def split_up(shard, dim, size):
    before, after = (shard.shape[:dim], shard.shape[dim + 1 :])
    return jnp.moveaxis(shard.reshape(*before, size, -1, *after), dim, 0)


def in_order(blocks, dim):
    dims = list(blocks.shape[1:])
    dims[dim] *= blocks.shape[0]
    return jnp.moveaxis(blocks, 0, dim).reshape(dims)


def turned_blocks(blocks, axes, turns):
    dims = [lax.axis_size(a) for a in axes]
    blocks = blocks.reshape(*dims, *blocks.shape[1:])
    for k in turns:
        blocks = lax.all_to_all(blocks, axes[k], split_axis=k, concat_axis=k, tiled=True)
    return blocks.reshape(-1, *blocks.shape[len(axes) :])


def two_step_exchange(shard, groups, turns, split_dim, concat_dim):
    size = lax.axis_size(groups[0]) * lax.axis_size(groups[1])
    blocks = split_up(shard, split_dim, size)
    return in_order(turned_blocks(blocks, groups, turns), concat_dim)


def reduced_to_own(blocks, axes, turns):
    dims = [lax.axis_size(a) for a in axes]
    blocks = blocks.reshape(*dims, *blocks.shape[1:])
    blocks = blocks.transpose(*turns, *range(len(axes), blocks.ndim))
    blocks = blocks.reshape(-1, *blocks.shape[len(axes) :])
    for k in turns:
        blocks = lax.psum_scatter(blocks, axes[k], scatter_dimension=0, tiled=True)
    return blocks[0]


def sum_by_axis(shard, axes, turns, dim):
    size = lax.axis_size(axes)
    return reduced_to_own(split_up(shard, dim, size), axes, turns)


def sum_by_axis_2(total, axes):
    for axis in axes:
        total = lax.psum_scatter(total, axis, scatter_dimension=0, tiled=True)
    return total


def one_axis_at_a_time(shard, axes):
    return functools.reduce(lax.psum, axes, shard)


def local(latents, shift, scale_mod, head_weight, bank):
    samples = latents.shape[0]
    width = head_weight.shape[1]
    feats = latents.astype(jnp.float32)
    inverse = lax.rsqrt(jnp.mean(feats * feats, axis=1, keepdims=True) + 1e-06)
    hidden = (
        feats * inverse * (1.0 + scale_mod.astype(jnp.float32)) + shift.astype(jnp.float32)
    ).astype(jnp.bfloat16)
    columns = two_step_exchange(hidden, ("gen_0", "gen_1"), (1, 0), 1, 0)
    partial_embed = jnp.dot(columns, head_weight, preferred_element_type=jnp.float32)
    embed = sum_by_axis(partial_embed, GEN, (1, 0), 0)
    length = jnp.sqrt(jnp.sum(embed * embed, axis=1, keepdims=True) + 1e-06)
    unit_exact = embed / length
    unit = unit_exact.astype(jnp.bfloat16)
    members = lax.all_gather(unit, BANK, axis=0, tiled=True)
    batch = members.shape[0]
    scores = jnp.dot(unit, members.T, preferred_element_type=jnp.float32)
    own_column = lax.axis_index(BANK) * samples + lax.broadcasted_iota(jnp.int32, scores.shape, 0)
    same = lax.broadcasted_iota(jnp.int32, scores.shape, 1) == own_column
    pair_weight = jnp.where(same, jnp.float32(0.0), jnp.exp(kernel_scale * scores)).astype(
        jnp.bfloat16
    )
    near = jnp.dot(pair_weight, members, preferred_element_type=jnp.float32) / (batch - 1)
    bank_f = bank.astype(jnp.float32)
    bank_unit = (bank_f / jnp.sqrt(jnp.sum(bank_f * bank_f, axis=1, keepdims=True) + 1e-06)).astype(
        jnp.bfloat16
    )
    bank_scores = jnp.dot(members, bank_unit.T, preferred_element_type=jnp.float32)
    bank_weight = jnp.exp(kernel_scale * bank_scores).astype(jnp.bfloat16)
    far = sum_by_axis_2(
        jnp.dot(bank_weight, bank_unit, preferred_element_type=jnp.float32), BANK
    ) / (bank.shape[0] * lax.axis_size(BANK))
    proof = near - far
    radial = jnp.sum(unit_exact * proof, axis=1, keepdims=True)
    grad_embed = ((proof - unit_exact * radial) / length).astype(jnp.bfloat16)
    feature_cols = lax.all_to_all(hidden, GEN_BANK, split_axis=1, concat_axis=0, tiled=True)
    every_grad = lax.all_gather(grad_embed, GEN_BANK, axis=0, tiled=True)
    gradient = lax.dot_general(
        feature_cols, every_grad, (((0,), (0,)), ((), ())), preferred_element_type=jnp.float32
    )
    squares = one_axis_at_a_time(jnp.sum(gradient * gradient), GEN_BANK)
    entries = hidden.shape[1] * width
    return gradient * lax.rsqrt(squares / entries + 1e-06)


def solution(mesh):
    torus = Mesh(
        mesh.devices.reshape(2, 2, 4, 4, 2), ("gen_0", "gen_1", "bank_0", "bank_1", "bank_2")
    )
    return jax.shard_map(
        local,
        mesh=torus,
        in_specs=(
            P(GEN_BANK, None),
            P(GEN_BANK, None),
            P(GEN_BANK, None),
            P(GEN, None),
            P(BANK, None),
        ),
        out_specs=P(GEN_BANK, None),
        check_vma=False,
    )
```

profile of v0, /device:TPU:1, one launch (start us, length us, event | category | flops | bytes accessed | tf_op | source)
XLA Modules:
  0.0 685.4 jit_solution(4880624567774161361)
XLA Ops:
  6.5 0.0 copy-start
  6.5 0.0 reduce-scatter.6.cloned.1.call-start
  6.5 1.4 fusion.18
  7.9 1.7 fusion.21
  9.6 0.4 reshape.35
  10.0 0.2 copy.22
  10.2 5.2 all_to_all.29
  15.4 9.8 %all_to_all.30 = bf16[2,2,64,1024]{3,2,1,0:T(8,128)(2,1)S(1)} all-to-all(bf16[2,2,64,1024]{3,2,1,0:T(8,128)(2,1)S(1)} %copy.24), channel_id=1, replica_groups=mesh['gen_0'=2,'gen_1'=2,'bank_0'=4,'bank_1'=4,'bank_2'=2] {'gen_0'}, dimensions={0} | all-to-all | bytes 1048576 | tf_op jit(solution)/shard_map/all_to_all | solution.py:32
  25.2 0.0 copy-done
  25.3 0.7 fusion.12
  26.0 1.1 copy.25
  27.1 0.0 reduce-scatter.6.cloned.1.call-update
  27.1 0.0 reduce-scatter.8.cloned.1.call-start
  27.1 14.9 %reduce-scatter.6.cloned.1.call-done = f32[2,64,1024]{2,1,0:T(8,128)} async-done(((f32[4,64,1024]{2,1,0:T(8,128)}), f32[2,64,1024]{2,1,0:T(8,128)}) %reduce-scatter.6.cloned.1.call-update) | async-done | bytes 524304 | tf_op jit(solution)/shard_map/reduce_scatter | solution.py:48
  42.1 0.0 reduce-scatter.8.cloned.1.call-update
  42.1 0.0 all-gather.3.cloned.1.call-start
  42.2 20.3 %reduce-scatter.8.cloned.1.call-done = f32[1,64,1024]{2,1,0:T(8,128)} async-done(((f32[2,64,1024]{2,1,0:T(8,128)}), f32[1,64,1024]{2,1,0:T(8,128)}) %reduce-scatter.8.cloned.1.call-update) | async-done | bytes 262160 | tf_op jit(solution)/shard_map/reduce_scatter | solution.py:48
  62.4 1.1 fusion.22
  63.5 1.7 fusion.29
  65.2 0.0 all-gather.3.cloned.1.call-update
  65.2 0.2 reduce-scatter.10.cloned.1.call-start
  65.5 3.1 fusion
  68.6 77.3 %all-gather.3.cloned.1.call-done = bf16[2048,1024]{1,0:T(8,128)(2,1)} async-done(((bf16[64,1024]{1,0:T(8,128)(2,1)}), bf16[2048,1024]{1,0:T(8,128)(2,1)}) %all-gather.3.cloned.1.call-update) | async-done | bytes 4194320 | tf_op jit(solution)/shard_map/all_gather | solution.py:81
  145.9 26.1 %fusion.2 = f32[2048,1024]{1,0:T(8,128)} fusion(bf16[2048,1024]{1,0:T(8,128)(2,1)} %all-gather.3.cloned.1.call-done, bf16[2048,1024]{1,0:T(8,128)(2,1)} %param.9, f32[2048]{0:T(1024)S(1)} %add_sqrt_fusion), kind=kOutput, calls=%fused_computation.5 | convolution fusion | flops 17200840704 | bytes 16785408 | tf_op jit(solution)/shard_map/dot_general | solution.py:97
  172.0 0.0 copy-start.1
  172.0 0.0 reduce-scatter.10.cloned.1.call-update
  172.0 0.0 reduce-scatter.12.cloned.1.call-start
  172.1 80.7 %reduce-scatter.10.cloned.1.call-done = f32[512,1024]{1,0:T(8,128)} async-done(((f32[2048,1024]{1,0:T(8,128)}), f32[512,1024]{1,0:T(8,128)}) %reduce-scatter.10.cloned.1.call-update) | async-done | bytes 2097168 | tf_op jit(solution)/shard_map/reduce_scatter | solution.py:59
  252.7 0.0 reduce-scatter.12.cloned.1.call-update
  252.8 0.0 reduce-scatter.14.cloned.1.call-start
  252.8 31.5 %reduce-scatter.12.cloned.1.call-done = f32[128,1024]{1,0:T(8,128)} async-done(((f32[512,1024]{1,0:T(8,128)}), f32[128,1024]{1,0:T(8,128)}) %reduce-scatter.12.cloned.1.call-update) | async-done | bytes 524304 | tf_op jit(solution)/shard_map/reduce_scatter | solution.py:59
  284.3 0.0 reduce-scatter.14.cloned.1.call-update
  284.3 0.0 all-gather.5.cloned.1.call-start
  284.4 20.4 %reduce-scatter.14.cloned.1.call-done = f32[64,1024]{1,0:T(8,128)} async-done(((f32[128,1024]{1,0:T(8,128)}), f32[64,1024]{1,0:T(8,128)}) %reduce-scatter.14.cloned.1.call-update) | async-done | bytes 262160 | tf_op jit(solution)/shard_map/reduce_scatter | solution.py:59
  304.8 0.0 copy-done.1
  304.8 5.8 multiply_reduce_fusion
  310.6 0.8 divide_convert_fusion
  311.4 0.0 all-gather.5.cloned.1.call-update
  311.4 1.3 copy.20
  312.7 2.3 reshape.39
  315.1 23.6 %all_to_all.31 = bf16[128,2,1024]{2,1,0:T(2,128)(2,1)S(1)} all-to-all(bf16[128,2,1024]{2,1,0:T(2,128)(2,1)S(1)} %reshape.39), channel_id=1, replica_groups=mesh['gen_0'=2,'gen_1'=2,'bank_0'=4,'bank_1'=4,'bank_2'=2] {'gen_0','gen..., dimensions={0} | all-to-all | bytes 1048576 | tf_op jit(solution)/shard_map/all_to_all | solution.py:102
  338.7 1.6 reshape.40
  340.3 1.3 bitcast_bitcast_fusion
  341.6 1.4 copy.21
  343.0 2.1 all_to_all.23
  345.0 290.8 %all-gather.5.cloned.1.call-done = bf16[8192,1024]{1,0:T(8,128)(2,1)} async-done(((bf16[64,1024]{1,0:T(8,128)(2,1)}), bf16[8192,1024]{1,0:T(8,128)(2,1)}) %all-gather.5.cloned.1.call-update) | async-done | bytes 16777232 | tf_op jit(solution)/shard_map/all_gather | solution.py:103
  635.9 9.4 %multiply_reduce_fusion.1 = (f32[]{:T(128)}, f32[32,1024]{1,0:T(8,128)S(1)}) fusion(bf16[8192,32]{0,1:T(8,128)(2,1)S(1)} %all_to_all.23, bf16[8192,1024]{1,0:T(8,128)(2,1)} %all-gather.5.cloned.1.call-done), kind=kOutput, calls=%fused_computation.32 | convolution fusion | flops 536936448 | bytes 17432580 | tf_op jit(solution)/shard_map/dot_general | solution.py:104
  645.2 4.4 psum.35
  649.6 4.2 psum.36
  653.8 8.6 %psum.37 = f32[]{:T(128)} all-reduce(f32[]{:T(128)} %psum.36), channel_id=1, replica_groups=mesh['gen_0'=2,'gen_1'=2,'bank_0'=4,'bank_1'=4,'bank_2'=2] {'bank_0'}, use_global_device_ids=true, to_apply=%region_12.13 | all-reduce | flops 1 | bytes 8 | tf_op jit(solution)/shard_map/psum | solution.py:64
  662.4 8.9 %psum.38 = f32[]{:T(128)} all-reduce(f32[]{:T(128)} %psum.37), channel_id=1, replica_groups=mesh['gen_0'=2,'gen_1'=2,'bank_0'=4,'bank_1'=4,'bank_2'=2] {'bank_1'}, use_global_device_ids=true, to_apply=%region_13.14 | all-reduce | flops 1 | bytes 8 | tf_op jit(solution)/shard_map/psum | solution.py:64
  671.3 5.9 psum.39
  677.9 0.7 broadcast_multiply_fusion
  (6 shorter events, 0.1 us)
Async XLA Ops:
  6.5 18.7 %copy-start = (bf16[1024,1024]{1,0:T(8,128)(2,1)S(1)}, bf16[1024,1024]{1,0:T(8,128)(2,1)}, u32[]{:S(2)}) copy-start(bf16[1024,1024]{1,0:T(8,128)(2,1)} %param.8) | copy-start | bytes 6291460
  6.5 35.5 %reduce-scatter.6.cloned.1.call-start = ((), (), s32[]{:S(2)}) async-start(), calls=%async_computation.8 | async-start | bytes 1572864 | tf_op jit(solution)/shard_map/reduce_scatter | solution.py:48
  27.1 35.3 %reduce-scatter.8.cloned.1.call-start = ((), (), s32[]{:S(2)}) async-start(), calls=%async_computation.9 | async-start | bytes 786432 | tf_op jit(solution)/shard_map/reduce_scatter | solution.py:48
  42.1 103.8 %all-gather.3.cloned.1.call-start = ((), (), s32[]{:S(2)}) async-start(), calls=%async_computation.10 | async-start | bytes 4325376 | tf_op jit(solution)/shard_map/all_gather | solution.py:81
  65.2 187.5 %reduce-scatter.10.cloned.1.call-start = ((), (), s32[]{:S(2)}) async-start(), calls=%async_computation.11 | async-start | bytes 10485760 | tf_op jit(solution)/shard_map/reduce_scatter | solution.py:59
  172.0 132.8 %copy-start.1 = (f32[1,64,1024]{2,1,0:T(8,128)S(1)}, f32[1,64,1024]{2,1,0:T(8,128)}, u32[]{:S(2)}) copy-start(f32[1,64,1024]{2,1,0:T(8,128)} %reduce-scatter.8.cloned.1.call-done) | copy-start | bytes 786436
  172.0 112.3 %reduce-scatter.12.cloned.1.call-start = ((), (), s32[]{:S(2)}) async-start(), calls=%async_computation.12 | async-start | bytes 2621440 | tf_op jit(solution)/shard_map/reduce_scatter | solution.py:59
  252.8 52.0 %reduce-scatter.14.cloned.1.call-start = ((), (), s32[]{:S(2)}) async-start(), calls=%async_computation.13 | async-start | bytes 786432 | tf_op jit(solution)/shard_map/reduce_scatter | solution.py:59
  284.3 351.5 %all-gather.5.cloned.1.call-start = ((), (), s32[]{:S(2)}) async-start(), calls=%async_computation.14 | async-start | bytes 16908288 | tf_op jit(solution)/shard_map/all_gather | solution.py:103
Sparse Core Ops, SparseCore 0:
  27.2 14.8 reduce-scatter.5
  44.4 17.9 reduce-scatter.7
  65.5 80.3 all-gather.2
  172.1 80.5 reduce-scatter.9
  255.0 29.2 reduce-scatter.11
  286.5 18.2 reduce-scatter.13
  311.5 324.2 all-gather.4
where the time goes:
time: 691 us; the launch traced here: 685 us
  waiting for transfers between devices  536 us (78%)
  blocking collectives  70.6 us (10%)
  matrix products  41.9 us (6%)
  between operations  14.3 us (2%)
  local copies, waits for them, and re-layouts  11.7 us (2%)
  other arithmetic  10.4 us (2%)
    all_gather x1, waiting for transfers between devices, local(): every_grad = lax.all_gather(grad_embed, GEN_BANK, axis=0, tiled=True)  291 us
    reduce_scatter x3, waiting for transfers between devices, sum_by_axis_2(): total = lax.psum_scatter(total, axis, scatter_dimension=0, tiled=True)  133 us
    all_gather x1, waiting for transfers between devices, local(): members = lax.all_gather(unit, BANK, axis=0, tiled=True)  77.3 us
    reduce_scatter x2, waiting for transfers between devices, reduced_to_own(): blocks = lax.psum_scatter(blocks, axes[k], scatter_dimension=0, tiled=True)  35.2 us
    psum x5, blocking collectives, one_axis_at_a_time(): return functools.reduce(lax.psum, axes, shard)  32 us
    dot_general x1, matrix products, local(): jnp.dot(bank_weight, bank_unit, preferred_element_type=jnp.float32)  26.1 us
    all_to_all x1, blocking collectives, local(): lax.all_to_all(hidden, GEN_BANK, split_axis=1, concat_axis=0, tiled=True)  23.6 us
    all_to_all x2, blocking collectives, turned_blocks(): lax.all_to_all(blocks, axes[k], split_axis=k, concat_axis=k, tiled=True)  15 us
  transfers between devices with their start and end apart: 7, of which 7 were waited for; matrix products, arithmetic and copies ran while one was open for 2% of the time, Pallas kernels for 0%

commit v1 on v0

v1 whole, which is shorter than its diff:
```python
import functools

import jax
import jax.numpy as jnp
from jax import lax
from jax.experimental import pallas as pl
from jax.experimental.pallas import tpu as pltpu
from jax.sharding import Mesh
from jax.sharding import PartitionSpec as P

AXES = ("xl", "c", "z", "y", "xh")
MESH = pl.DeviceIdType.MESH
F32 = jnp.float32
BF16 = jnp.bfloat16
KERNEL_SCALE = 32.0
N_PLANE = 16
CHUNKS = 4
NEAREST = sorted(range(1, 16), key=lambda k: min(k // 4, 4 - k // 4) + min(k % 4, 4 - k % 4))


def kernel(
    lat, shift, scale, hw_hbm, bank_hbm, out,
    hid, lhs, w, ret, er, ue, lens, units, mate, bu, acc, wide, landed, hs, cols, grads, part, xin,
    grad, q1, q1in, q2, q2in, loc, ss, rs,
):
    xl, c, z, y, xh = (lax.axis_index(a) for a in AXES)
    me = z * 4 + y
    rows, width = ret.shape
    half = hid.shape[2]
    strip = half // 2
    brows = bu.shape[1]
    samples = acc.shape[0]

    ids = iter(range(ss.shape[0]))

    def remote(src, dst, device):
        i = next(ids)
        return pltpu.make_async_remote_copy(
            src_ref=src, dst_ref=dst, send_sem=ss.at[i], recv_sem=rs.at[i],
            device_id=device, device_id_type=MESH,
        )

    def on_plane(k):
        tz, ty = lax.rem(z + k // 4, 4), lax.rem(y + k % 4, 4)
        return {"z": tz, "y": ty}, tz * 4 + ty

    def on_line(k):
        return {
            "xl": 1 - xl if k & 1 else xl,
            "c": 1 - c if k & 2 else c,
            "xh": 1 - xh if k & 4 else xh,
        }

    core = {"c": 1 - c}
    pair = {"xl": 1 - xl}
    cut = {"xl": 1 - xl, "xh": 1 - xh}
    far_mate = {"xh": 1 - xh}

    load_w = pltpu.make_async_copy(hw_hbm, w.at[c], loc.at[0])
    load_w.start()
    load_b = pltpu.make_async_copy(bank_hbm, bu.at[0], loc.at[1])
    load_b.start()

    barrier = pltpu.get_barrier_semaphore()
    for k in range(1, N_PLANE):
        pl.semaphore_signal(barrier, inc=1, device_id=on_plane(k)[0], device_id_type=MESH)
    for k in range(1, 8):
        pl.semaphore_signal(barrier, inc=1, device_id=on_line(k), device_id_type=MESH)

    def modulate(i, _):
        r = pl.ds(pl.multiple_of(i * 16, 16), 16)
        f = lat[r, :].astype(F32)
        inverse = lax.rsqrt(jnp.mean(f * f, axis=1, keepdims=True) + 1e-06)
        h = (f * inverse * (1.0 + scale[r, :].astype(F32)) + shift[r, :].astype(F32)).astype(BF16)
        hid[0, r, :] = h[:, :half]
        hid[1, r, :] = h[:, half:]
        return 0

    lax.fori_loop(0, rows // 16, modulate, 0)
    pl.semaphore_wait(barrier, N_PLANE - 1 + 7)

    send_h = remote(hid.at[1 - xl], lhs.at[pl.ds(rows, rows)], pair)
    send_h.start()
    load_w.wait()
    send_w = remote(w.at[c], w.at[c], core)
    send_w.start()
    lhs[:rows] = hid[xl]

    load_b.wait()

    def unit_rows(i, _):
        r = pl.ds(pl.multiple_of(i * 64, 64), 64)
        b = bu[0, r, :].astype(F32)
        bu[0, r, :] = (b * lax.rsqrt(jnp.sum(b * b, axis=1, keepdims=True) + 1e-06)).astype(BF16)
        return 0

    lax.fori_loop(0, brows // 64, unit_rows, 0)
    per = brows // 2 // CHUNKS
    send_b, pass_b, pieces = [], [], []
    for i in range(CHUNKS):
        mine = pl.ds(pl.multiple_of(c * (brows // 2) + i * per, per), per)
        theirs = pl.ds(pl.multiple_of((1 - c) * (brows // 2) + i * per, per), per)
        pieces.append((mine, theirs))
        send_b.append(remote(bu.at[0, mine], bu.at[1, mine], cut))
        send_b[-1].start()
        pass_b.append(remote(bu.at[1, mine], bu.at[1, mine], core))

    send_w.wait()
    send_h.wait()
    emb = jnp.dot(lhs[...], w[...].reshape(half, width), preferred_element_type=F32)
    ret[...] = emb[rows:]
    ue[...] = emb[:rows]
    send_e = remote(ret, er, pair)
    send_e.start()
    for p in range(N_PLANE // 2):
        for g in range(4):
            o = (g % 2) * strip + p * 128
            hs[p, :, g * 128 : (g + 1) * 128] = hid[g // 2, :, o : o + 128]
    send_e.wait()
    embed = ue[...] + er[...]
    length = jnp.sqrt(jnp.sum(embed * embed, axis=1, keepdims=True) + 1e-06)
    lens[...] = length
    unit = embed / length
    ue[...] = unit
    units[me] = unit.astype(BF16)
    send_u = []
    for k in NEAREST:
        device, _ = on_plane(k)
        send_u.append(remote(units.at[me], units.at[me], device))
        send_u[-1].start()
    send_m = remote(units.at[me], mate, far_mate)
    send_m.start()
    send_c = []
    cols[me] = hs[me // 2]
    for k in NEAREST:
        device, m = on_plane(k)
        send_c.append(remote(hs.at[m // 2], cols.at[me], device))
        send_c[-1].start()
    for copy in send_u:
        copy.wait()

    tile = 256

    def weigh(slot, r, first):
        def step(i, _):
            s = pl.ds(pl.multiple_of(i * tile, tile), tile)
            u = units[pl.ds(i * (tile // rows), tile // rows)].reshape(tile, width)
            b = bu[slot, r, :]
            scores = lax.dot_general(u, b, (((1,), (1,)), ((), ())), preferred_element_type=F32)
            weight = jnp.exp(KERNEL_SCALE * scores).astype(BF16)
            total = jnp.dot(weight, b, preferred_element_type=F32)
            acc[s, :] = total if first else acc[s, :] + total
            return 0

        lax.fori_loop(0, samples // tile, step, 0)

    size = 512
    weigh(0, pl.ds(0, size), True)

    def own_rest(j, _):
        weigh(0, pl.ds(pl.multiple_of(j * size, size), size), False)
        return 0

    lax.fori_loop(1, brows // size, own_rest, 0)
    for i in range(CHUNKS):
        send_b[i].wait()
        pass_b[i].start()
        weigh(1, pieces[i][0], False)
        pass_b[i].wait()
        weigh(1, pieces[i][1], False)

    send_m.wait()
    batch = 2 * samples

    def near(i, _):
        s = pl.ds(pl.multiple_of(i * tile, tile), tile)
        u = units[pl.ds(i * (tile // rows), tile // rows)].reshape(tile, width)
        total = jnp.zeros((tile, width), F32)
        for t, own in ((units[me], True), (mate[...], False)):
            scores = lax.dot_general(u, t, (((1,), (1,)), ((), ())), preferred_element_type=F32)
            weight = jnp.exp(KERNEL_SCALE * scores)
            if own:
                row = i * tile + lax.broadcasted_iota(jnp.int32, weight.shape, 0)
                column = me * rows + lax.broadcasted_iota(jnp.int32, weight.shape, 1)
                weight = jnp.where(row == column, F32(0.0), weight)
            total = total + jnp.dot(weight.astype(BF16), t, preferred_element_type=F32)
        proof = total * (1.0 / (batch - 1)) - acc[s, :] * (1.0 / (brows * 32))
        acc[s, :] = proof
        wide[pl.ds(i * (tile // rows), tile // rows)] = proof.astype(BF16).reshape(
            tile // rows, rows, width
        )
        return 0

    lax.fori_loop(0, samples // tile, near, 0)

    send_p = []
    for k in NEAREST:
        device, m = on_plane(k)
        send_p.append(remote(wide.at[m], landed.at[k - 1], device))
        send_p[-1].start()
    proof = acc[pl.ds(pl.multiple_of(me * rows, rows), rows), :]
    for copy, k in zip(send_p, NEAREST):
        copy.wait()
        proof = proof + landed[k - 1].astype(F32)
    unit = ue[...]
    radial = jnp.sum(unit * proof, axis=1, keepdims=True)
    grads[me] = ((proof - unit * radial) / lens[...]).astype(BF16)

    send_g = []
    for k in NEAREST:
        device, _ = on_plane(k)
        send_g.append(remote(grads.at[me], grads.at[me], device))
        send_g[-1].start()
    for copy in send_c:
        copy.wait()
    for copy in send_g:
        copy.wait()

    feats = cols[...].reshape(samples, 512)
    part[...] = lax.dot_general(
        feats, grads[...].reshape(samples, width), (((0,), (0,)), ((), ())),
        preferred_element_type=F32,
    )
    lane = lax.rem(y, 2) * 64

    def block(axl, ac, axh):
        return pl.ds(pl.multiple_of((axl * 2 + ac) * 128 + lane + axh * 32, 32), 32)

    send_x = []
    for k in range(1, 8):
        to = on_line(k)
        send_x.append(remote(part.at[block(to["xl"], to["c"], to["xh"])], xin.at[k - 1], to))
        send_x[-1].start()
    total = part[block(xl, c, xh), :]
    for k in range(1, 8):
        send_x[k - 1].wait()
        total = total + xin[k - 1]
    grad[...] = total
    squares = total * total
    fold = jnp.zeros((8, 128), F32)
    for a in range(4):
        for b in range(width // 128):
            fold = fold + squares[a * 8 : a * 8 + 8, b * 128 : b * 128 + 128]
    q1[...] = fold
    send_q = []
    for k in range(1, 8):
        send_q.append(remote(q1, q1in.at[k - 1], on_line(k)))
        send_q[-1].start()
    for k in range(1, 8):
        send_q[k - 1].wait()
        fold = fold + q1in[k - 1]
    q2[...] = fold
    send_q = []
    for k in range(1, N_PLANE):
        send_q.append(remote(q2, q2in.at[k - 1], on_plane(k)[0]))
        send_q[-1].start()
    for k in range(1, N_PLANE):
        send_q[k - 1].wait()
        fold = fold + q2in[k - 1]
    mean = jnp.sum(jnp.sum(fold, axis=1, keepdims=True), axis=0, keepdims=True) / (
        4 * strip * width
    )
    out[...] = grad[...] * lax.rsqrt(mean + 1e-06)


def local(latents, shift, scale_mod, head_weight, bank):
    rows, depth = latents.shape
    width = head_weight.shape[1]
    brows = bank.shape[0]
    samples = rows * N_PLANE
    vmem = pl.BlockSpec(memory_space=pltpu.VMEM)
    hbm = pl.BlockSpec(memory_space=pl.ANY)
    n_sems = 3 + 2 * CHUNKS + 1 + 15 * 5 + 7 * 2
    return pl.pallas_call(
        kernel,
        out_shape=jax.ShapeDtypeStruct((depth // 128, width), F32),
        in_specs=[vmem, vmem, vmem, hbm, hbm],
        out_specs=vmem,
        scratch_shapes=[
            pltpu.VMEM((2, rows, depth // 2), BF16),
            pltpu.VMEM((2 * rows, depth // 2), BF16),
            pltpu.VMEM((2, depth // 4, width), BF16),
            pltpu.VMEM((rows, width), F32),
            pltpu.VMEM((rows, width), F32),
            pltpu.VMEM((rows, width), F32),
            pltpu.VMEM((rows, 1), F32),
            pltpu.VMEM((N_PLANE, rows, width), BF16),
            pltpu.VMEM((rows, width), BF16),
            pltpu.VMEM((2, brows, width), BF16),
            pltpu.VMEM((samples, width), F32),
            pltpu.VMEM((N_PLANE, rows, width), BF16),
            pltpu.VMEM((N_PLANE - 1, rows, width), BF16),
            pltpu.VMEM((N_PLANE // 2, rows, 512), BF16),
            pltpu.VMEM((N_PLANE, rows, 512), BF16),
            pltpu.VMEM((N_PLANE, rows, width), BF16),
            pltpu.VMEM((512, width), F32),
            pltpu.VMEM((7, 32, width), F32),
            pltpu.VMEM((32, width), F32),
            pltpu.VMEM((8, 128), F32),
            pltpu.VMEM((7, 8, 128), F32),
            pltpu.VMEM((8, 128), F32),
            pltpu.VMEM((15, 8, 128), F32),
            pltpu.SemaphoreType.DMA((2,)),
            pltpu.SemaphoreType.DMA((n_sems,)),
            pltpu.SemaphoreType.DMA((n_sems,)),
        ],
        compiler_params=pltpu.CompilerParams(
            collective_id=0, has_side_effects=True, vmem_limit_bytes=60 * 1024 * 1024
        ),
        name="mmd_step",
    )(latents, shift, scale_mod, head_weight, bank)


def solution(mesh):
    torus = Mesh(mesh.devices.reshape(2, 2, 4, 4, 2), AXES)
    return jax.shard_map(
        local,
        mesh=torus,
        in_specs=(P(AXES, None), P(AXES, None), P(AXES, None), P(("xl", "c"), None), P(("z", "y", "xh"), None)),
        out_specs=P(AXES, None),
        check_vma=False,
    )
```

time: 691 us -> 171 us (0.25)
  waiting for transfers between devices: 536 us -> 0 us
  Pallas kernels: 0 us -> 169 us
  blocking collectives: 70.6 us -> 0 us
  matrix products: 41.9 us -> 0 us
  between operations: 14.3 us -> 0.01 us
  other arithmetic: 10.4 us -> 0 us
  local copies, waits for them, and re-layouts: 11.7 us -> 1.57 us
    all_gather x2 -> x0, waiting for transfers between devices: 368 us -> none  [the longest x1 291 us: local(): every_grad = lax.all_gather(grad_embed, GEN_BANK, axis=0, tiled=True)]
    pallas_call x0 -> x1, Pallas kernels: none -> 169 us  [local(): pl.pallas_call(kernel, out_shape=jax.ShapeDtypeStruct((depth // 128, widt...]
    reduce_scatter x5 -> x0, waiting for transfers between devices: 168 us -> none  [the longest x3 133 us: sum_by_axis_2(): total = lax.psum_scatter(total, axis, scatter_dimension=0, tiled=True)]
    dot_general x4 -> x0, matrix products: 41.9 us -> none  [the longest x1 26.1 us: local(): jnp.dot(bank_weight, bank_unit, preferred_element_type=jnp.float32)]
    all_to_all x3 -> x0, blocking collectives: 38.6 us -> none  [the longest x1 23.6 us: local(): lax.all_to_all(hidden, GEN_BANK, split_axis=1, concat_axis=0, tiled=True)]
    psum x5 -> x0, blocking collectives: 32 us -> none  [one_axis_at_a_time(): return functools.reduce(lax.psum, axes, shard)]
  transfers between devices with their start and end apart: 7 -> 0, of which waited for: 7 -> 0; matrix products, arithmetic and copies ran while one was open for 2% -> 0% of each run, Pallas kernels for 0% -> 0%
where the time goes in v1:
time: 171 us; the launch traced here: 170 us
  Pallas kernels  169 us (99%)
    pallas_call x1, Pallas kernels, local(): pl.pallas_call(kernel, out_shape=jax.ShapeDtypeStruct((depth // 128, widt...  169 us

profile of v1, /device:TPU:1, one launch (start us, length us, event | category | flops | bytes accessed | tf_op | source)
XLA Modules:
  0.0 170.5 jit_solution(13948680661727851956)
XLA Ops:
  0.0 168.9 %mmd_step.1 = f32[32,1024]{1,0:T(8,128)} custom-call(bf16[64,4096]{1,0:T(8,128)(2,1)} %lat.1, bf16[64,4096]{1,0:T(8,128)(2,1)} %shift.1, bf16[64,4096]{1,0:T(8,128)(2,1)} %scale.1, bf16[1024,1024]{1,0:T(8,128)(2,1)} %hw_hbm.1, bf16[2048,1024]{1,0:T(8,128)(2,1)} %bank_hbm.1), custom_call_target="tpu_custom_call" | custom-call | tf_op jit(solution)/shard_map/mmd_step/pallas_call | solution.py:274
  168.9 1.6 copy.7

commit v2 on v1

v2 whole, which is shorter than its diff:
```python
import functools

import jax
import jax.numpy as jnp
from jax import lax
from jax.experimental import pallas as pl
from jax.experimental.pallas import tpu as pltpu
from jax.sharding import Mesh
from jax.sharding import PartitionSpec as P

AXES = ("xl", "c", "z", "y", "xh")
MESH = pl.DeviceIdType.MESH
F32 = jnp.float32
BF16 = jnp.bfloat16
KERNEL_SCALE = 32.0
N_PLANE = 16
CHUNKS = 4
NEAREST = sorted(range(1, 16), key=lambda k: min(k // 4, 4 - k // 4) + min(k % 4, 4 - k % 4))


def kernel(
    lat, shift, scale, hw_hbm, bank_hbm, out,
    hid, lhs, w, ret, er, ue, lens, units, pairt, bu, acc, wide, landed, hs, cols, grads, part, mine,
    xin, grad, q1, q1in, q2, q2in, loc, ss, rs,
):
    xl, c, z, y, xh = (lax.axis_index(a) for a in AXES)
    me = z * 4 + y
    rows, width = ret.shape
    half = hid.shape[2]
    strip = half // 2
    brows = bu.shape[1] * bu.shape[2]
    quarter = bu.shape[2]
    tiles, _, trows = units.shape[:3]
    tile = N_PLANE * trows
    hrows = rows // 2

    ids = iter(range(ss.shape[0]))

    def remote(src, dst, device):
        i = next(ids)
        return pltpu.make_async_remote_copy(
            src_ref=src, dst_ref=dst, send_sem=ss.at[i], recv_sem=rs.at[i],
            device_id=device, device_id_type=MESH,
        )

    def send(src, dst, device):
        copy = remote(src, dst, device)
        copy.start()
        return copy

    def on_plane(k):
        tz, ty = lax.rem(z + k // 4, 4), lax.rem(y + k % 4, 4)
        return {"z": tz, "y": ty}, tz * 4 + ty

    def on_line(k):
        return {
            "xl": 1 - xl if k & 1 else xl,
            "c": 1 - c if k & 2 else c,
            "xh": 1 - xh if k & 4 else xh,
        }

    core = {"c": 1 - c}
    pair = {"xl": 1 - xl}
    cut = {"xl": 1 - xl, "xh": 1 - xh}
    far_mate = {"xh": 1 - xh}

    load_w = pltpu.make_async_copy(hw_hbm, w.at[c], loc.at[0])
    load_w.start()
    load_b = []
    for q in range(4):
        load_b.append(
            pltpu.make_async_copy(bank_hbm.at[pl.ds(q * quarter, quarter)], bu.at[0, q], loc.at[1 + q])
        )
        load_b[-1].start()

    barrier = pltpu.get_barrier_semaphore()
    for k in range(1, N_PLANE):
        pl.semaphore_signal(barrier, inc=1, device_id=on_plane(k)[0], device_id_type=MESH)
    for k in range(1, 8):
        pl.semaphore_signal(barrier, inc=1, device_id=on_line(k), device_id_type=MESH)

    def modulate(i, _):
        r = pl.ds(pl.multiple_of(i * 16, 16), 16)
        f = lat[r, :].astype(F32)
        inverse = lax.rsqrt(jnp.mean(f * f, axis=1, keepdims=True) + 1e-06)
        h = (f * inverse * (1.0 + scale[r, :].astype(F32)) + shift[r, :].astype(F32)).astype(BF16)
        hid[0, r, :] = h[:, :half]
        hid[1, r, :] = h[:, half:]
        return 0

    lax.fori_loop(0, rows // 16, modulate, 0)
    pl.semaphore_wait(barrier, N_PLANE - 1 + 7)

    upper, lower = pl.ds(0, hrows), pl.ds(hrows, hrows)
    send_h = [
        send(hid.at[1 - xl, upper], lhs.at[pl.ds(rows, hrows)], pair),
        send(hid.at[1 - xl, lower], lhs.at[pl.ds(rows + hrows, hrows)], cut),
    ]
    load_w.wait()
    send_w = send(w.at[c], w.at[c], core)
    lhs[:rows] = hid[xl]
    for p in range(N_PLANE // 2):
        for g in range(4):
            o = (g % 2) * strip + p * 128
            for h in range(2):
                hs[p, h, :, g * 128 : (g + 1) * 128] = hid[
                    g // 2, h * hrows : (h + 1) * hrows, o : o + 128
                ]
    send_c = []
    for k in NEAREST:
        device, m = on_plane(k)
        send_c.append(send(hs.at[m // 2], cols.at[:, me], device))
    for h in range(2):
        cols[h, me] = hs[me // 2, h]

    def unit_rows(q, lo, hi):
        def step(i, _):
            r = pl.ds(pl.multiple_of(i * 64, 64), 64)
            b = bu[0, q, r, :].astype(F32)
            bu[0, q, r, :] = (b * lax.rsqrt(jnp.sum(b * b, axis=1, keepdims=True) + 1e-06)).astype(BF16)
            return 0

        lax.fori_loop(lo // 64, hi // 64, step, 0)

    for q in range(4):
        load_b[q].wait()
    gone = (1 - xl) * 2 + c
    own_q = xl * 2 + c
    pair_q = (1 - xl) * 2 + c
    per = quarter // CHUNKS

    def piece(i):
        return pl.ds(i * per, per)

    send_b = [remote(bu.at[0, gone, piece(i)], bu.at[1, gone, piece(i)], cut) for i in range(CHUNKS)]
    pass_core = [remote(bu.at[1, own_q, piece(i)], bu.at[1, own_q, piece(i)], core) for i in range(CHUNKS)]
    pass_pair = [remote(bu.at[1, own_q, piece(i)], bu.at[1, own_q, piece(i)], pair) for i in range(CHUNKS)]
    pass_last = [remote(bu.at[1, pair_q, piece(i)], bu.at[1, pair_q, piece(i)], core) for i in range(CHUNKS)]
    unit_rows(gone, 0, quarter)
    send_b[0].start()
    for k in range(1, 4):
        unit_rows(lax.rem(gone + k, 4), 0, quarter)

    send_w.wait()
    for copy in send_h:
        copy.wait()
    emb = jnp.dot(lhs[...], w[...].reshape(half, width), preferred_element_type=F32)
    ret[...] = emb[rows:]
    ue[...] = emb[:rows]
    send_e = [
        send(ret.at[upper], er.at[upper], pair),
        send(ret.at[lower], er.at[lower], cut),
    ]
    for i in range(1, CHUNKS):
        send_b[i].start()
    for copy in send_e:
        copy.wait()
    embed = ue[...] + er[...]
    length = jnp.sqrt(jnp.sum(embed * embed, axis=1, keepdims=True) + 1e-06)
    lens[...] = length
    unit = embed / length
    ue[...] = unit
    unit_b = unit.astype(BF16)
    pairt[:rows] = unit_b
    for j in range(tiles):
        units[j, me] = unit_b[j * trows : (j + 1) * trows]
    send_u = [
        [send(units.at[j, me], units.at[j, me], on_plane(k)[0]) for k in NEAREST] for j in range(tiles)
    ]
    send_m = send(pairt.at[pl.ds(0, rows)], pairt.at[pl.ds(rows, rows)], far_mate)

    def pass_on(i):
        send_b[i].wait()
        pass_core[i].start()
        pass_pair[i].start()

    def pass_again(i):
        pass_pair[i].wait()
        pass_last[i].start()

    def weigh(slot, j, order, first):
        u = units[j].reshape(tile, width)
        total = None if first else acc[j]
        for q in order:
            b = bu[slot, q]
            scores = lax.dot_general(u, b, (((1,), (1,)), ((), ())), preferred_element_type=F32)
            weight = jnp.exp(KERNEL_SCALE * scores).astype(BF16)
            term = jnp.dot(weight, b, preferred_element_type=F32)
            total = term if total is None else total + term
        acc[j] = total

    batch = 2 * tiles * tile

    def finish(j):
        u = units[j].reshape(tile, width)
        t = pairt[...]
        scores = lax.dot_general(u, t, (((1,), (1,)), ((), ())), preferred_element_type=F32)
        row = lax.broadcasted_iota(jnp.int32, scores.shape, 0) - me * trows
        column = lax.broadcasted_iota(jnp.int32, scores.shape, 1) - j * trows
        same = jnp.logical_and(row == column, jnp.logical_and(column >= 0, column < trows))
        weight = jnp.where(same, F32(0.0), jnp.exp(KERNEL_SCALE * scores)).astype(BF16)
        total = jnp.dot(weight, t, preferred_element_type=F32)
        proof = total * (1.0 / (batch - 1)) - acc[j] * (1.0 / (brows * 32))
        acc[j] = proof
        wide[j] = proof.astype(BF16).reshape(N_PLANE, trows, width)
        sends = []
        for k in NEAREST:
            device, m = on_plane(k)
            sends.append(send(wide.at[j, m], landed.at[j, k - 1], device))
        return sends

    own = (0, 1, 2, 3)
    other = (own_q, xl * 2 + 1 - c, pair_q, (1 - xl) * 2 + 1 - c)
    pass_on(0)
    pass_on(1)
    for copy in send_u[0]:
        copy.wait()
    weigh(0, 0, own, True)
    pass_on(2)
    pass_again(0)
    for copy in send_u[1]:
        copy.wait()
    weigh(0, 1, own, True)
    pass_on(3)
    pass_again(1)
    for copy in send_u[2]:
        copy.wait()
    weigh(0, 2, own, True)
    pass_again(2)
    pass_again(3)
    for i in range(CHUNKS):
        pass_core[i].wait()
    for i in range(CHUNKS):
        pass_last[i].wait()
    weigh(1, 0, other, False)
    send_m.wait()
    send_p = [finish(0)]
    weigh(1, 1, other, False)
    send_p.append(finish(1))
    weigh(1, 2, other, False)
    send_p.append(finish(2))
    for copy in send_u[3]:
        copy.wait()
    weigh(0, 3, own, True)
    weigh(1, 3, other, False)
    send_p.append(finish(3))

    for j in range(tiles):
        proof = acc[j, pl.ds(pl.multiple_of(me * trows, trows), trows), :]
        for copy, k in zip(send_p[j], NEAREST):
            copy.wait()
            proof = proof + landed[j, k - 1].astype(F32)
        r = slice(j * trows, (j + 1) * trows)
        unit = ue[r, :]
        radial = jnp.sum(unit * proof, axis=1, keepdims=True)
        o = (j * trows) % hrows
        grads[j * trows // hrows, me, o : o + trows, :] = (
            (proof - unit * radial) / lens[r, :]
        ).astype(BF16)

    def along(h, second, d):
        if (h == 0) != second:
            return {"z": lax.rem(z + d, 4)}
        return {"y": lax.rem(y + d, 4)}

    def source(h, d):
        if h == 0:
            return lax.rem(z + 4 - d, 4) * 4 + y
        return z * 4 + lax.rem(y + 4 - d, 4)

    steps = (1, 3, 2)
    first = {}
    for d in steps:
        for h in range(2):
            first[h, d] = send(grads.at[h, me], grads.at[h, me], along(h, False, d))
    second = []
    for d in steps:
        for h in range(2):
            second.append(send(grads.at[h, me], grads.at[h, me], along(h, True, d)))
    for d in steps:
        for h in range(2):
            first[h, d].wait()
            m = source(h, d)
            for e in steps:
                second.append(send(grads.at[h, m], grads.at[h, m], along(h, True, e)))
    for copy in send_c:
        copy.wait()
    for copy in second:
        copy.wait()

    feats = cols[...].reshape(N_PLANE * rows, 512)
    part[...] = lax.dot_general(
        feats, grads[...].reshape(N_PLANE * rows, width), (((0,), (0,)), ((), ())),
        preferred_element_type=F32,
    )
    lane = lax.rem(y, 2) * 64

    def strip_of(axl, ac):
        return pl.ds(pl.multiple_of((axl * 2 + ac) * 128 + lane, 64), 64)

    swap = [send(part.at[strip_of(a, 1 - c)], mine.at[a], core) for a in range(2)]
    for a in range(2):
        swap[a].wait()
        mine[2 + a] = mine[a] + part[strip_of(a, c), :]
    send_x = []
    for k in (1, 5, 4):
        to = on_line(k)
        block = mine.at[2 + to["xl"], pl.ds(pl.multiple_of(to["xh"] * 32, 32), 32)]
        send_x.append(send(block, xin.at[len(send_x)], to))
    total = mine[2 + xl, pl.ds(pl.multiple_of(xh * 32, 32), 32), :]
    for i in range(3):
        send_x[i].wait()
        total = total + xin[i]
    grad[...] = total
    squares = total * total
    fold = jnp.zeros((8, 128), F32)
    for a in range(4):
        for b in range(width // 128):
            fold = fold + squares[a * 8 : a * 8 + 8, b * 128 : b * 128 + 128]
    q1[...] = fold
    send_q = []
    for k in range(1, 8):
        send_q.append(send(q1, q1in.at[k - 1], on_line(k)))
    for k in range(1, 8):
        send_q[k - 1].wait()
        fold = fold + q1in[k - 1]
    q2[...] = fold
    send_q = []
    for k in range(1, N_PLANE):
        send_q.append(send(q2, q2in.at[k - 1], on_plane(k)[0]))
    for k in range(1, N_PLANE):
        send_q[k - 1].wait()
        fold = fold + q2in[k - 1]
    mean = jnp.sum(jnp.sum(fold, axis=1, keepdims=True), axis=0, keepdims=True) / (
        4 * strip * width
    )
    out[...] = grad[...] * lax.rsqrt(mean + 1e-06)


def local(latents, shift, scale_mod, head_weight, bank):
    rows, depth = latents.shape
    width = head_weight.shape[1]
    brows = bank.shape[0]
    vmem = pl.BlockSpec(memory_space=pltpu.VMEM)
    hbm = pl.BlockSpec(memory_space=pl.ANY)
    n_sems = 5 + 4 * CHUNKS + 15 + 60 + 1 + 60 + 30 + 5 + 7 + 15
    return pl.pallas_call(
        kernel,
        out_shape=jax.ShapeDtypeStruct((depth // 128, width), F32),
        in_specs=[vmem, vmem, vmem, hbm, hbm],
        out_specs=vmem,
        scratch_shapes=[
            pltpu.VMEM((2, rows, depth // 2), BF16),
            pltpu.VMEM((2 * rows, depth // 2), BF16),
            pltpu.VMEM((2, depth // 4, width), BF16),
            pltpu.VMEM((rows, width), F32),
            pltpu.VMEM((rows, width), F32),
            pltpu.VMEM((rows, width), F32),
            pltpu.VMEM((rows, 1), F32),
            pltpu.VMEM((4, N_PLANE, rows // 4, width), BF16),
            pltpu.VMEM((2 * rows, width), BF16),
            pltpu.VMEM((2, 4, brows // 4, width), BF16),
            pltpu.VMEM((4, N_PLANE * rows // 4, width), F32),
            pltpu.VMEM((4, N_PLANE, rows // 4, width), BF16),
            pltpu.VMEM((4, N_PLANE - 1, rows // 4, width), BF16),
            pltpu.VMEM((N_PLANE // 2, 2, rows // 2, 512), BF16),
            pltpu.VMEM((2, N_PLANE, rows // 2, 512), BF16),
            pltpu.VMEM((2, N_PLANE, rows // 2, width), BF16),
            pltpu.VMEM((512, width), F32),
            pltpu.VMEM((4, 64, width), F32),
            pltpu.VMEM((3, 32, width), F32),
            pltpu.VMEM((32, width), F32),
            pltpu.VMEM((8, 128), F32),
            pltpu.VMEM((7, 8, 128), F32),
            pltpu.VMEM((8, 128), F32),
            pltpu.VMEM((15, 8, 128), F32),
            pltpu.SemaphoreType.DMA((5,)),
            pltpu.SemaphoreType.DMA((n_sems,)),
            pltpu.SemaphoreType.DMA((n_sems,)),
        ],
        compiler_params=pltpu.CompilerParams(
            collective_id=0, has_side_effects=True, vmem_limit_bytes=60 * 1024 * 1024
        ),
        name="mmd_step",
    )(latents, shift, scale_mod, head_weight, bank)


def solution(mesh):
    torus = Mesh(mesh.devices.reshape(2, 2, 4, 4, 2), AXES)
    return jax.shard_map(
        local,
        mesh=torus,
        in_specs=(P(AXES, None), P(AXES, None), P(AXES, None), P(("xl", "c"), None), P(("z", "y", "xh"), None)),
        out_specs=P(AXES, None),
        check_vma=False,
    )
```

time: 171 us -> 123 us (0.72)
  Pallas kernels: 169 us -> 121 us
    pallas_call x1, Pallas kernels: 169 us -> 121 us  [local(): pl.pallas_call(kernel, out_shape=jax.ShapeDtypeStruct((depth // 128, widt...]
where the time goes in v2:
time: 123 us
  Pallas kernels  121 us (98%)
  local copies, waits for them, and re-layouts  1.57 us (1%)
    pallas_call x1, Pallas kernels, local(): pl.pallas_call(kernel, out_shape=jax.ShapeDtypeStruct((depth // 128, widt...  121 us

profile of v2, /device:TPU:1, one launch (start us, length us, event | category | flops | bytes accessed | tf_op | source)
XLA Modules:
  0.0 122.9 jit_solution(761167533786921891)
XLA Ops:
  0.0 121.4 %mmd_step.1 = f32[32,1024]{1,0:T(8,128)} custom-call(bf16[64,4096]{1,0:T(8,128)(2,1)} %lat.1, bf16[64,4096]{1,0:T(8,128)(2,1)} %shift.1, bf16[64,4096]{1,0:T(8,128)(2,1)} %scale.1, bf16[1024,1024]{1,0:T(8,128)(2,1)} %hw_hbm.1, bf16[2048,1024]{1,0:T(8,128)(2,1)} %bank_hbm.1), custom_call_target="tpu_custom_call" | custom-call | tf_op jit(solution)/shard_map/mmd_step/pallas_call | solution.py:347
  121.4 1.6 %copy.7 = f32[32,1024]{1,0:T(8,128)} copy(f32[32,1024]{1,0:T(8,128)} %mmd_step.1) | data formatting | bytes 262144

commit v3 on v2

v3 whole, which is shorter than its diff:
```python
import functools

import jax
import jax.numpy as jnp
from jax import lax
from jax.experimental import pallas as pl
from jax.experimental.pallas import tpu as pltpu
from jax.sharding import Mesh
from jax.sharding import PartitionSpec as P

AXES = ("xl", "c", "z", "y", "xh")
MESH = pl.DeviceIdType.MESH
F32 = jnp.float32
BF16 = jnp.bfloat16
KERNEL_SCALE = 32.0
N_PLANE = 16
CHUNKS = 8
NEAREST = sorted(range(1, 16), key=lambda k: min(k // 4, 4 - k // 4) + min(k % 4, 4 - k % 4))


def kernel(
    lat, shift, scale, hw_hbm, bank_hbm, grad, factor,
    hid, lhs, w, ret, er, ue, lens, units, pairt, bu, acc, wide, landed, mids, landed2, keep, hs, cols, grads, part, mine,
    xin, q1, q1in, q2, q2in, loc, ss, rs,
):
    xl, c, z, y, xh = (lax.axis_index(a) for a in AXES)
    me = z * 4 + y
    rows, width = ret.shape
    half = hid.shape[2]
    strip = half // 2
    brows = bu.shape[1] * bu.shape[2]
    quarter = bu.shape[2]
    tiles, _, trows = units.shape[:3]
    tile = N_PLANE * trows
    hrows = rows // 2

    ids = iter(range(ss.shape[0]))

    def remote(src, dst, device):
        i = next(ids)
        return pltpu.make_async_remote_copy(
            src_ref=src, dst_ref=dst, send_sem=ss.at[i], recv_sem=rs.at[i],
            device_id=device, device_id_type=MESH,
        )

    def send(src, dst, device):
        copy = remote(src, dst, device)
        copy.start()
        return copy

    def on_plane(k):
        tz, ty = lax.rem(z + k // 4, 4), lax.rem(y + k % 4, 4)
        return {"z": tz, "y": ty}, tz * 4 + ty

    def on_line(k):
        return {
            "xl": 1 - xl if k & 1 else xl,
            "c": 1 - c if k & 2 else c,
            "xh": 1 - xh if k & 4 else xh,
        }

    core = {"c": 1 - c}
    pair = {"xl": 1 - xl}
    cut = {"xl": 1 - xl, "xh": 1 - xh}
    far_mate = {"xh": 1 - xh}

    gone = (1 - xl) * 2 + c
    load_b = []
    for k in range(4):
        q = lax.rem(gone + k, 4)
        rows_q = pl.ds(pl.multiple_of(q * quarter, quarter), quarter)
        load_b.append(pltpu.make_async_copy(bank_hbm.at[rows_q], bu.at[0, q], loc.at[1 + k]))
    load_w = pltpu.make_async_copy(hw_hbm, w.at[c], loc.at[0])
    load_b[0].start()
    load_w.start()
    for k in range(1, 4):
        load_b[k].start()

    barrier = pltpu.get_barrier_semaphore()
    for k in range(1, N_PLANE):
        pl.semaphore_signal(barrier, inc=1, device_id=on_plane(k)[0], device_id_type=MESH)
    for k in range(1, 8):
        pl.semaphore_signal(barrier, inc=1, device_id=on_line(k), device_id_type=MESH)

    def modulate(i, _):
        r = pl.ds(pl.multiple_of(i * 16, 16), 16)
        f = lat[r, :].astype(F32)
        inverse = lax.rsqrt(jnp.mean(f * f, axis=1, keepdims=True) + 1e-06)
        h = (f * inverse * (1.0 + scale[r, :].astype(F32)) + shift[r, :].astype(F32)).astype(BF16)
        hid[0, r, :] = h[:, :half]
        hid[1, r, :] = h[:, half:]
        return 0

    lax.fori_loop(0, rows // 16, modulate, 0)
    for p in range(N_PLANE // 2):
        for g in range(4):
            o = (g % 2) * strip + p * 128
            for j in range(tiles):
                hs[p, j, :, g * 128 : (g + 1) * 128] = hid[
                    g // 2, j * trows : (j + 1) * trows, o : o + 128
                ]
    for j in range(tiles):
        cols[j, me] = hs[me // 2, j]
    lhs[:rows] = hid[xl]

    def unit_rows(q):
        def step(i, _):
            r = pl.ds(pl.multiple_of(i * 64, 64), 64)
            b = bu[0, q, r, :].astype(F32)
            bu[0, q, r, :] = (b * lax.rsqrt(jnp.sum(b * b, axis=1, keepdims=True) + 1e-06)).astype(BF16)
            return 0

        lax.fori_loop(0, quarter // 64, step, 0)

    load_b[0].wait()
    own_q = xl * 2 + c
    pair_q = (1 - xl) * 2 + c
    per = quarter // CHUNKS
    unit_rows(gone)
    pl.semaphore_wait(barrier, N_PLANE - 1 + 7)

    upper, lower = pl.ds(0, hrows), pl.ds(hrows, hrows)
    send_h = [
        send(hid.at[1 - xl, upper], lhs.at[pl.ds(rows, hrows)], pair),
        send(hid.at[1 - xl, lower], lhs.at[pl.ds(rows + hrows, hrows)], cut),
    ]
    load_w.wait()
    send_w = send(w.at[c], w.at[c], core)

    def piece(i):
        return pl.ds(i * per, per)

    send_b = [remote(bu.at[0, gone, piece(i)], bu.at[1, gone, piece(i)], cut) for i in range(CHUNKS)]
    pass_core = [remote(bu.at[1, own_q, piece(i)], bu.at[1, own_q, piece(i)], core) for i in range(CHUNKS)]
    pass_pair = [remote(bu.at[1, own_q, piece(i)], bu.at[1, own_q, piece(i)], pair) for i in range(CHUNKS)]
    pass_last = [remote(bu.at[1, pair_q, piece(i)], bu.at[1, pair_q, piece(i)], core) for i in range(CHUNKS)]
    send_b[0].start()
    send_c = []
    for k in NEAREST:
        device, m = on_plane(k)
        send_c.append(send(hs.at[m // 2], cols.at[:, me], device))
    for k in range(1, 4):
        load_b[k].wait()
        unit_rows(lax.rem(gone + k, 4))

    send_w.wait()
    for copy in send_h:
        copy.wait()
    emb = jnp.dot(lhs[...], w[...].reshape(half, width), preferred_element_type=F32)
    ret[...] = emb[rows:]
    ue[...] = emb[:rows]
    send_e = [
        send(ret.at[upper], er.at[upper], pair),
        send(ret.at[lower], er.at[lower], cut),
    ]
    for i in range(1, CHUNKS):
        send_b[i].start()
    for copy in send_e:
        copy.wait()
    embed = ue[...] + er[...]
    length = jnp.sqrt(jnp.sum(embed * embed, axis=1, keepdims=True) + 1e-06)
    lens[...] = length
    unit = embed / length
    ue[...] = unit
    unit_b = unit.astype(BF16)
    pairt[:rows] = unit_b
    for j in range(tiles):
        units[j, me] = unit_b[j * trows : (j + 1) * trows]

    def along(h, second, d):
        if (h == 0) != second:
            return {"z": lax.rem(z + d, 4)}
        return {"y": lax.rem(y + d, 4)}

    def source(h, d):
        if h == 0:
            return lax.rem(z + 4 - d, 4) * 4 + y
        return z * 4 + lax.rem(y + 4 - d, 4)

    steps = (1, 3, 2)

    def gather(block):
        first, second = {}, []
        for d in steps:
            for h in range(2):
                first[h, d] = send(block(h, me), block(h, me), along(h, False, d))
        for d in steps:
            for h in range(2):
                second.append(send(block(h, me), block(h, me), along(h, True, d)))

        def forward():
            for d in steps:
                for h in range(2):
                    first[h, d].wait()
                    m = source(h, d)
                    for e in steps:
                        second.append(send(block(h, m), block(h, m), along(h, True, e)))

        def done():
            for copy in second:
                copy.wait()

        return forward, done

    def gather_units(j):
        return gather(lambda h, m: units.at[j, m, :, pl.ds(h * (width // 2), width // 2)])

    flows = [gather_units(0), gather_units(1)]

    def pass_on(i):
        send_b[i].wait()
        pass_core[i].start()
        pass_pair[i].start()

    def pass_again(i):
        pass_pair[i].wait()
        pass_last[i].start()

    def weigh(slot, j, order, first):
        u = units[j].reshape(tile, width)
        total = None if first else acc[j].reshape(tile, width)
        for q in order:
            b = bu[slot, q]
            scores = lax.dot_general(u, b, (((1,), (1,)), ((), ())), preferred_element_type=F32)
            weight = jnp.exp(KERNEL_SCALE * scores).astype(BF16)
            term = jnp.dot(weight, b, preferred_element_type=F32)
            total = term if total is None else total + term
        acc[j] = total.reshape(4, 4, trows, width)

    batch = 2 * tiles * tile

    def finish(j):
        u = units[j].reshape(tile, width)
        t = pairt[...]
        scores = lax.dot_general(u, t, (((1,), (1,)), ((), ())), preferred_element_type=F32)
        row = lax.broadcasted_iota(jnp.int32, scores.shape, 0) - me * trows
        column = lax.broadcasted_iota(jnp.int32, scores.shape, 1) - j * trows
        same = jnp.logical_and(row == column, jnp.logical_and(column >= 0, column < trows))
        weight = jnp.where(same, F32(0.0), jnp.exp(KERNEL_SCALE * scores)).astype(BF16)
        total = jnp.dot(weight, t, preferred_element_type=F32)
        proof = total * (1.0 / (batch - 1)) - acc[j].reshape(tile, width) * (1.0 / (brows * 32))
        proof = proof.reshape(4, 4, trows, width)
        acc[j] = proof
        wide[j] = proof.astype(BF16)
        sends = {}
        for d in steps:
            tz, ty = lax.rem(z + d, 4), lax.rem(y + d, 4)
            sends[0, d] = send(wide.at[j, tz, :, :, left], landed.at[j, 0, d - 1], {"z": tz})
            sends[1, d] = send(wide.at[j, :, ty, :, right], landed.at[j, 1, d - 1], {"y": ty})
        return sends

    left, right = pl.ds(0, width // 2), pl.ds(width // 2, width // 2)

    def middle(j, firsts):
        sends = []
        for h in range(2):
            part_sum = acc[j, z, :, :, left] if h == 0 else acc[j, :, y, :, right]
            for d in steps:
                firsts[h, d].wait()
                part_sum = part_sum + landed[j, h, d - 1].astype(F32)
            keep[...] = part_sum
            mids[j, h] = part_sum.astype(BF16)
            acc[j, 0, h, :, left] = keep[y if h == 0 else z]
            for e in steps:
                to = lax.rem((y if h == 0 else z) + e, 4)
                sends.append(
                    send(mids.at[j, h, to], landed2.at[j, h, e - 1], {"y": to} if h == 0 else {"z": to})
                )
        return sends

    def land(j, sends):
        for copy in sends:
            copy.wait()
        halves = []
        for h in range(2):
            own_sum = acc[j, 0, h, :, left]
            for e in steps:
                own_sum = own_sum + landed2[j, h, e - 1].astype(F32)
            halves.append(own_sum)
        proof = jnp.concatenate(halves, axis=1)
        r = slice(j * trows, (j + 1) * trows)
        unit = ue[r, :]
        radial = jnp.sum(unit * proof, axis=1, keepdims=True)
        grads[j, me] = ((proof - unit * radial) / lens[r, :]).astype(BF16)
        return gather(lambda h, m: grads.at[j, m, :, pl.ds(h * (width // 2), width // 2)])

    own = (0, 1, 2, 3)
    core_q = xl * 2 + 1 - c
    near_q = (own_q, core_q)
    late_q = (pair_q, (1 - xl) * 2 + 1 - c)
    pass_on(0)
    flows[0][0]()
    flows.append(gather_units(2))
    pass_on(1)
    flows[1][0]()
    flows.append(gather_units(3))
    pass_on(2)
    flows[0][1]()
    pass_on(3)
    weigh(0, 0, own, True)
    flows[2][0]()
    pass_on(4)
    pass_again(0)
    pass_again(1)
    flows[1][1]()
    weigh(0, 1, own, True)
    flows[3][0]()
    pass_on(5)
    pass_again(2)
    flows[2][1]()
    weigh(0, 2, own, True)
    pass_on(6)
    pass_again(3)
    flows[3][1]()
    weigh(0, 3, own, True)
    pass_on(7)
    send_m = send(pairt.at[pl.ds(0, rows)], pairt.at[pl.ds(rows, rows)], far_mate)
    pass_again(4)
    weigh(1, 2, (own_q,), False)
    weigh(1, 3, (own_q,), False)
    pass_again(5)
    for i in range(CHUNKS):
        pass_core[i].wait()
    weigh(1, 0, near_q, False)
    pass_again(6)
    weigh(1, 1, near_q, False)
    weigh(1, 2, (core_q,), False)
    weigh(1, 3, (core_q,), False)
    pass_again(7)
    for i in range(CHUNKS):
        pass_last[i].wait()
    send_m.wait()
    weigh(1, 0, late_q, False)
    send_p = [finish(0)]
    weigh(1, 1, late_q, False)
    send_p.append(finish(1))
    weigh(1, 2, late_q, False)
    send_p.append(finish(2))
    middles = [middle(0, send_p[0])]
    weigh(1, 3, late_q, False)
    send_p.append(finish(3))
    middles.append(middle(1, send_p[1]))
    spread = [land(0, middles[0])]
    middles.append(middle(2, send_p[2]))
    spread.append(land(1, middles[1]))
    middles.append(middle(3, send_p[3]))
    spread[0][0]()
    spread.append(land(2, middles[2]))
    spread[1][0]()
    spread.append(land(3, middles[3]))
    spread[2][0]()
    spread[3][0]()
    for copy in send_c:
        copy.wait()
    for j in range(tiles):
        spread[j][1]()

    feats = cols[...].reshape(N_PLANE * rows, 512)
    part[...] = lax.dot_general(
        feats, grads[...].reshape(N_PLANE * rows, width), (((0,), (0,)), ((), ())),
        preferred_element_type=F32,
    )
    lane = lax.rem(y, 2) * 64

    def strip_of(axl, ac):
        return pl.ds(pl.multiple_of((axl * 2 + ac) * 128 + lane, 64), 64)

    swap = [send(part.at[strip_of(a, 1 - c)], mine.at[a], core) for a in range(2)]
    for a in range(2):
        swap[a].wait()
        mine[2 + a] = mine[a] + part[strip_of(a, c), :]
    send_x = []
    for k in (1, 5, 4):
        to = on_line(k)
        block = mine.at[2 + to["xl"], pl.ds(pl.multiple_of(to["xh"] * 32, 32), 32)]
        send_x.append(send(block, xin.at[len(send_x)], to))
    total = mine[2 + xl, pl.ds(pl.multiple_of(xh * 32, 32), 32), :]
    for i in range(3):
        send_x[i].wait()
        total = total + xin[i]
    grad[...] = total
    squares = total * total
    fold = jnp.zeros((8, 128), F32)
    for a in range(4):
        for b in range(width // 128):
            fold = fold + squares[a * 8 : a * 8 + 8, b * 128 : b * 128 + 128]
    q1[...] = fold
    send_q = []
    for k in range(1, 8):
        send_q.append(send(q1, q1in.at[k - 1], on_line(k)))
    for k in range(1, 8):
        send_q[k - 1].wait()
        fold = fold + q1in[k - 1]
    q2[...] = fold
    send_q = []
    for k in range(1, N_PLANE):
        send_q.append(send(q2, q2in.at[k - 1], on_plane(k)[0]))
    for k in range(1, N_PLANE):
        send_q[k - 1].wait()
        fold = fold + q2in[k - 1]
    mean = jnp.sum(jnp.sum(fold, axis=1, keepdims=True), axis=0, keepdims=True) / (
        4 * strip * width
    )
    factor[...] = jnp.broadcast_to(lax.rsqrt(mean + 1e-06), factor.shape)


def local(latents, shift, scale_mod, head_weight, bank):
    rows, depth = latents.shape
    width = head_weight.shape[1]
    brows = bank.shape[0]
    vmem = pl.BlockSpec(memory_space=pltpu.VMEM)
    hbm = pl.BlockSpec(memory_space=pl.ANY)
    n_sems = 5 + 4 * CHUNKS + 15 + 4 * 30 + 1 + 4 * 12 + 4 * 30 + 5 + 7 + 15
    gradient, factor = pl.pallas_call(
        kernel,
        out_shape=(
            jax.ShapeDtypeStruct((depth // 128, width), F32),
            jax.ShapeDtypeStruct((1, 128), F32),
        ),
        in_specs=[vmem, vmem, vmem, hbm, hbm],
        out_specs=(vmem, vmem),
        scratch_shapes=[
            pltpu.VMEM((2, rows, depth // 2), BF16),
            pltpu.VMEM((2 * rows, depth // 2), BF16),
            pltpu.VMEM((2, depth // 4, width), BF16),
            pltpu.VMEM((rows, width), F32),
            pltpu.VMEM((rows, width), F32),
            pltpu.VMEM((rows, width), F32),
            pltpu.VMEM((rows, 1), F32),
            pltpu.VMEM((4, N_PLANE, rows // 4, width), BF16),
            pltpu.VMEM((2 * rows, width), BF16),
            pltpu.VMEM((2, 4, brows // 4, width), BF16),
            pltpu.VMEM((4, 4, 4, rows // 4, width), F32),
            pltpu.VMEM((4, 4, 4, rows // 4, width), BF16),
            pltpu.VMEM((4, 2, 3, 4, rows // 4, width // 2), BF16),
            pltpu.VMEM((4, 2, 4, rows // 4, width // 2), BF16),
            pltpu.VMEM((4, 2, 3, rows // 4, width // 2), BF16),
            pltpu.VMEM((4, rows // 4, width // 2), F32),
            pltpu.VMEM((N_PLANE // 2, 4, rows // 4, 512), BF16),
            pltpu.VMEM((4, N_PLANE, rows // 4, 512), BF16),
            pltpu.VMEM((4, N_PLANE, rows // 4, width), BF16),
            pltpu.VMEM((512, width), F32),
            pltpu.VMEM((4, 64, width), F32),
            pltpu.VMEM((3, 32, width), F32),
            pltpu.VMEM((8, 128), F32),
            pltpu.VMEM((7, 8, 128), F32),
            pltpu.VMEM((8, 128), F32),
            pltpu.VMEM((15, 8, 128), F32),
            pltpu.SemaphoreType.DMA((5,)),
            pltpu.SemaphoreType.DMA((n_sems,)),
            pltpu.SemaphoreType.DMA((n_sems,)),
        ],
        compiler_params=pltpu.CompilerParams(
            collective_id=0, has_side_effects=True, vmem_limit_bytes=60 * 1024 * 1024
        ),
        name="mmd_step",
    )(latents, shift, scale_mod, head_weight, bank)
    return gradient * factor[0, 0]


def solution(mesh):
    torus = Mesh(mesh.devices.reshape(2, 2, 4, 4, 2), AXES)
    return jax.shard_map(
        local,
        mesh=torus,
        in_specs=(P(AXES, None), P(AXES, None), P(AXES, None), P(("xl", "c"), None), P(("z", "y", "xh"), None)),
        out_specs=P(AXES, None),
        check_vma=False,
    )
```

time: 123 us -> 114 us (0.927)
  Pallas kernels: 121 us -> 111 us
  other arithmetic: 0 us -> 2.25 us
  local copies, waits for them, and re-layouts: 1.57 us -> 0 us
    pallas_call x1, Pallas kernels: 121 us -> 111 us  [local(): pl.pallas_call(kernel, out_shape=(jax.ShapeDtypeStruct((depth // 128, wid...]
    mul x0 -> x1, other arithmetic: none -> 2.25 us  [local(): return gradient * factor[0, 0]]
    unnamed x1 -> x0, local copies, waits for them, and re-layouts: 1.57 us -> none
where the time goes in v3:
time: 114 us; the launch traced here: 113 us
  Pallas kernels  111 us (97%)
  other arithmetic  2.25 us (2%)
    pallas_call x1, Pallas kernels, local(): pl.pallas_call(kernel, out_shape=(jax.ShapeDtypeStruct((depth // 128, wid...  111 us

profile of v3, /device:TPU:1, one launch (start us, length us, event | category | flops | bytes accessed | tf_op | source)
XLA Modules:
  0.0 113.5 jit_solution(4744717942548743963)
XLA Ops:
  0.0 111.2 %mmd_step.1 = (f32[32,1024]{1,0:T(8,128)}, f32[1,128]{1,0:T(1,128)}) custom-call(bf16[64,4096]{1,0:T(8,128)(2,1)} %lat.1, bf16[64,4096]{1,0:T(8,128)(2,1)} %shift.1, bf16[64,4096]{1,0:T(8,128)(2,1)} %scale.1, bf16[1024,1024]{1,0:T(8,128)(2,1)} %hw_hbm.1, bf16[2048,1024]{1,0:T(8,128)(2,1)} %bank_hbm.1), custom_call_target="tpu_custom_call" | custom-call | tf_op jit(solution)/shard_map/mmd_step/pallas_call | solution.py:414
  111.2 2.3 %broadcast_multiply_fusion = f32[32,1024]{1,0:T(8,128)} fusion(f32[32,1024]{1,0:T(8,128)} %get-tuple-element.7, f32[]{:T(128)} %bitcast.2), kind=kLoop, calls=%fused_computation | loop fusion | flops 32768 | bytes 262148 | tf_op jit(solution)/shard_map/mul | solution.py:458

commit v4 on v3

--- a/solution.py
+++ b/solution.py
@@ -21,7 +21,7 @@
 def kernel(
     lat, shift, scale, hw_hbm, bank_hbm, grad, factor,
     hid, lhs, w, ret, er, ue, lens, units, pairt, bu, acc, wide, landed, mids, landed2, keep, hs, cols, grads, part, mine,
-    xin, q1, q1in, q2, q2in, loc, ss, rs,
+    xin, xout, q1, q1in, q2, q2in, loc, ss, rs,
 ):
     xl, c, z, y, xh = (lax.axis_index(a) for a in AXES)
     me = z * 4 + y
@@ -202,6 +202,42 @@
 
         return forward, done
 
+    def gather_relay(block, size):
+        first, second, last = {}, {}, []
+        for d in steps:
+            for h in range(2):
+                first[h, d] = send(block(h, me, 0, size), block(h, me, 0, size), along(h, False, d))
+        for e in (1, 3):
+            for h in range(2):
+                second[h, 0, e] = send(block(h, me, 0, size), block(h, me, 0, size), along(h, True, e))
+
+        def forward():
+            for d in steps:
+                for h in range(2):
+                    first[h, d].wait()
+                    m = source(h, d)
+                    for e in (1, 3):
+                        second[h, d, e] = send(
+                            block(h, m, 0, size), block(h, m, 0, size), along(h, True, e)
+                        )
+
+        def relay():
+            for d in (0,) + steps:
+                for e in (1, 3):
+                    for h in range(2):
+                        second[h, d, e].wait()
+                        dz, dy = (d, e) if h == 0 else (e, d)
+                        m = lax.rem(z + 4 - dz, 4) * 4 + lax.rem(y + 4 - dy, 4)
+                        o = 0 if e == 1 else size // 2
+                        half_block = block(h, m, o, size // 2)
+                        last.append(send(half_block, half_block, along(h, True, e)))
+
+        def done():
+            for copy in last:
+                copy.wait()
+
+        return forward, relay, done
+
     def gather_units(j):
         return gather(lambda h, m: units.at[j, m, :, pl.ds(h * (width // 2), width // 2)])
 
@@ -282,11 +318,12 @@
         unit = ue[r, :]
         radial = jnp.sum(unit * proof, axis=1, keepdims=True)
         grads[j, me] = ((proof - unit * radial) / lens[r, :]).astype(BF16)
-        return gather(lambda h, m: grads.at[j, m, :, pl.ds(h * (width // 2), width // 2)])
+        return gather_relay(
+            lambda h, m, o, n: grads.at[j, m, :, pl.ds(h * (width // 2) + o, n)], width // 2
+        )
 
     own = (0, 1, 2, 3)
     core_q = xl * 2 + 1 - c
-    near_q = (own_q, core_q)
     late_q = (pair_q, (1 - xl) * 2 + 1 - c)
     pass_on(0)
     flows[0][0]()
@@ -319,14 +356,16 @@
     weigh(1, 2, (own_q,), False)
     weigh(1, 3, (own_q,), False)
     pass_again(5)
+    weigh(1, 0, (own_q,), False)
+    weigh(1, 1, (own_q,), False)
+    pass_again(6)
     for i in range(CHUNKS):
         pass_core[i].wait()
-    weigh(1, 0, near_q, False)
-    pass_again(6)
-    weigh(1, 1, near_q, False)
+    weigh(1, 0, (core_q,), False)
+    weigh(1, 1, (core_q,), False)
+    pass_again(7)
     weigh(1, 2, (core_q,), False)
     weigh(1, 3, (core_q,), False)
-    pass_again(7)
     for i in range(CHUNKS):
         pass_last[i].wait()
     send_m.wait()
@@ -347,43 +386,52 @@
     spread[0][0]()
     spread.append(land(2, middles[2]))
     spread[1][0]()
+    spread[0][1]()
     spread.append(land(3, middles[3]))
     spread[2][0]()
+    spread[1][1]()
     spread[3][0]()
+    spread[2][1]()
+    spread[3][1]()
     for copy in send_c:
         copy.wait()
     for j in range(tiles):
-        spread[j][1]()
-
-    feats = cols[...].reshape(N_PLANE * rows, 512)
-    part[...] = lax.dot_general(
-        feats, grads[...].reshape(N_PLANE * rows, width), (((0,), (0,)), ((), ())),
-        preferred_element_type=F32,
-    )
+        spread[j][2]()
+
+    feats = cols[...].reshape(N_PLANE * rows, 512).T
     lane = lax.rem(y, 2) * 64
 
     def strip_of(axl, ac):
         return pl.ds(pl.multiple_of((axl * 2 + ac) * 128 + lane, 64), 64)
 
-    swap = [send(part.at[strip_of(a, 1 - c)], mine.at[a], core) for a in range(2)]
-    for a in range(2):
-        swap[a].wait()
-        mine[2 + a] = mine[a] + part[strip_of(a, c), :]
+    swap = []
+    for side in (left, right):
+        samples_grads = grads[:, :, :, side].reshape(N_PLANE * rows, width // 2)
+        part[:, side] = jnp.dot(feats, samples_grads, preferred_element_type=F32)
+        swap.append([send(part.at[strip_of(a, 1 - c), side], mine.at[a, :, side], core) for a in range(2)])
+    here = pl.ds(pl.multiple_of(xh * 32, 32), 32)
     send_x = []
-    for k in (1, 5, 4):
-        to = on_line(k)
-        block = mine.at[2 + to["xl"], pl.ds(pl.multiple_of(to["xh"] * 32, 32), 32)]
-        send_x.append(send(block, xin.at[len(send_x)], to))
-    total = mine[2 + xl, pl.ds(pl.multiple_of(xh * 32, 32), 32), :]
-    for i in range(3):
-        send_x[i].wait()
-        total = total + xin[i]
-    grad[...] = total
-    squares = total * total
+    for h, side in enumerate((left, right)):
+        for a in range(2):
+            swap[h][a].wait()
+            total = mine[a, :, side] + part[strip_of(a, c), side]
+            mine[a, :, side] = total
+            xout[h, a] = total.astype(BF16)
+        for k in (1, 5, 4):
+            to = on_line(k)
+            block = xout.at[h, to["xl"], pl.ds(pl.multiple_of(to["xh"] * 32, 32), 32)]
+            send_x.append(send(block, xin.at[len(send_x)], to))
     fold = jnp.zeros((8, 128), F32)
-    for a in range(4):
-        for b in range(width // 128):
-            fold = fold + squares[a * 8 : a * 8 + 8, b * 128 : b * 128 + 128]
+    for h, side in enumerate((left, right)):
+        total = mine[xl, here, side]
+        for i in range(3):
+            send_x[h * 3 + i].wait()
+            total = total + xin[h * 3 + i].astype(F32)
+        grad[:, side] = total
+        squares = total * total
+        for a in range(4):
+            for b in range(width // 256):
+                fold = fold + squares[a * 8 : a * 8 + 8, b * 128 : b * 128 + 128]
     q1[...] = fold
     send_q = []
     for k in range(1, 8):
@@ -410,7 +458,7 @@
     brows = bank.shape[0]
     vmem = pl.BlockSpec(memory_space=pltpu.VMEM)
     hbm = pl.BlockSpec(memory_space=pl.ANY)
-    n_sems = 5 + 4 * CHUNKS + 15 + 4 * 30 + 1 + 4 * 12 + 4 * 30 + 5 + 7 + 15
+    n_sems = 5 + 4 * CHUNKS + 15 + 4 * 30 + 1 + 4 * 12 + 4 * 38 + 10 + 7 + 15
     gradient, factor = pl.pallas_call(
         kernel,
         out_shape=(
@@ -440,8 +488,9 @@
             pltpu.VMEM((4, N_PLANE, rows // 4, 512), BF16),
             pltpu.VMEM((4, N_PLANE, rows // 4, width), BF16),
             pltpu.VMEM((512, width), F32),
-            pltpu.VMEM((4, 64, width), F32),
-            pltpu.VMEM((3, 32, width), F32),
+            pltpu.VMEM((2, 64, width), F32),
+            pltpu.VMEM((6, 32, width // 2), BF16),
+            pltpu.VMEM((2, 2, 64, width // 2), BF16),
             pltpu.VMEM((8, 128), F32),
             pltpu.VMEM((7, 8, 128), F32),
             pltpu.VMEM((8, 128), F32),

time: 114 us -> 111 us (0.974)
  Pallas kernels: 111 us -> 109 us
    pallas_call x1, Pallas kernels: 111 us -> 109 us  [local(): pl.pallas_call(kernel, out_shape=(jax.ShapeDtypeStruct((depth // 128, wid...]
where the time goes in v4:
time: 111 us
  Pallas kernels  109 us (98%)
  other arithmetic  2.25 us (2%)
    pallas_call x1, Pallas kernels, local(): pl.pallas_call(kernel, out_shape=(jax.ShapeDtypeStruct((depth // 128, wid...  109 us
    mul x1, other arithmetic, local(): return gradient * factor[0, 0]  2.25 us

profile of v4, /device:TPU:1, one launch (start us, length us, event | category | flops | bytes accessed | tf_op | source)
XLA Modules:
  0.0 111.1 jit_solution(4247734692267291599)
XLA Ops:
  0.0 108.8 %mmd_step.1 = (f32[32,1024]{1,0:T(8,128)}, f32[1,128]{1,0:T(1,128)}) custom-call(bf16[64,4096]{1,0:T(8,128)(2,1)} %lat.1, bf16[64,4096]{1,0:T(8,128)(2,1)} %shift.1, bf16[64,4096]{1,0:T(8,128)(2,1)} %scale.1, bf16[1024,1024]{1,0:T(8,128)(2,1)} %hw_hbm.1, bf16[2048,1024]{1,0:T(8,128)(2,1)} %bank_hbm.1), custom_call_target="tpu_custom_call" | custom-call | tf_op jit(solution)/shard_map/mmd_step/pallas_call | solution.py:462
  108.8 2.3 %broadcast_multiply_fusion = f32[32,1024]{1,0:T(8,128)} fusion(f32[32,1024]{1,0:T(8,128)} %get-tuple-element.7, f32[]{:T(128)} %bitcast.2), kind=kLoop, calls=%fused_computation | loop fusion | flops 32768 | bytes 262148 | tf_op jit(solution)/shard_map/mul | solution.py:507

commit v5 on v4

--- a/solution.py
+++ b/solution.py
@@ -19,8 +19,8 @@
 
 
 def kernel(
-    lat, shift, scale, hw_hbm, bank_hbm, grad, factor,
-    hid, lhs, w, ret, er, ue, lens, units, pairt, bu, acc, wide, landed, mids, landed2, keep, hs, cols, grads, part, mine,
+    lat_hbm, shift_hbm, scale_hbm, hw_hbm, bank_hbm, grad, factor,
+    lat, shift, scale, hid, lhs, w, ret, er, ue, lens, units, pairt, bu, acc, wide, landed, mids, landed2, keep, hs, cols, grads, part, mine,
     xin, xout, q1, q1in, q2, q2in, loc, ss, rs,
 ):
     xl, c, z, y, xh = (lax.axis_index(a) for a in AXES)
@@ -64,6 +64,18 @@
     cut = {"xl": 1 - xl, "xh": 1 - xh}
     far_mate = {"xh": 1 - xh}
 
+    load_f = [
+        pltpu.make_async_copy(src, dst, loc.at[5 + n])
+        for n, (src, dst) in enumerate(((lat_hbm, lat), (shift_hbm, shift), (scale_hbm, scale)))
+    ]
+    for copy in load_f:
+        copy.start()
+    barrier = pltpu.get_barrier_semaphore()
+    for k in range(1, N_PLANE):
+        pl.semaphore_signal(barrier, inc=1, device_id=on_plane(k)[0], device_id_type=MESH)
+    for k in range(1, 8):
+        pl.semaphore_signal(barrier, inc=1, device_id=on_line(k), device_id_type=MESH)
+
     gone = (1 - xl) * 2 + c
     load_b = []
     for k in range(4):
@@ -76,12 +88,6 @@
     for k in range(1, 4):
         load_b[k].start()
 
-    barrier = pltpu.get_barrier_semaphore()
-    for k in range(1, N_PLANE):
-        pl.semaphore_signal(barrier, inc=1, device_id=on_plane(k)[0], device_id_type=MESH)
-    for k in range(1, 8):
-        pl.semaphore_signal(barrier, inc=1, device_id=on_line(k), device_id_type=MESH)
-
     def modulate(i, _):
         r = pl.ds(pl.multiple_of(i * 16, 16), 16)
         f = lat[r, :].astype(F32)
@@ -91,6 +97,8 @@
         hid[1, r, :] = h[:, half:]
         return 0
 
+    for copy in load_f:
+        copy.wait()
     lax.fori_loop(0, rows // 16, modulate, 0)
     for p in range(N_PLANE // 2):
         for g in range(4):
@@ -318,6 +326,8 @@
         unit = ue[r, :]
         radial = jnp.sum(unit * proof, axis=1, keepdims=True)
         grads[j, me] = ((proof - unit * radial) / lens[r, :]).astype(BF16)
+        if j == tiles - 1:
+            return gather(lambda h, m: grads.at[j, m, :, pl.ds(h * (width // 2), width // 2)])
         return gather_relay(
             lambda h, m, o, n: grads.at[j, m, :, pl.ds(h * (width // 2) + o, n)], width // 2
         )
@@ -342,15 +352,17 @@
     flows[1][1]()
     weigh(0, 1, own, True)
     flows[3][0]()
-    pass_on(5)
     pass_again(2)
     flows[2][1]()
-    weigh(0, 2, own, True)
+    weigh(0, 2, (0, 1), True)
+    pass_on(5)
+    weigh(0, 2, (2, 3), False)
     pass_on(6)
     pass_again(3)
     flows[3][1]()
-    weigh(0, 3, own, True)
+    weigh(0, 3, (0, 1), True)
     pass_on(7)
+    weigh(0, 3, (2, 3), False)
     send_m = send(pairt.at[pl.ds(0, rows)], pairt.at[pl.ds(rows, rows)], far_mate)
     pass_again(4)
     weigh(1, 2, (own_q,), False)
@@ -358,9 +370,9 @@
     pass_again(5)
     weigh(1, 0, (own_q,), False)
     weigh(1, 1, (own_q,), False)
-    pass_again(6)
     for i in range(CHUNKS):
         pass_core[i].wait()
+    pass_again(6)
     weigh(1, 0, (core_q,), False)
     weigh(1, 1, (core_q,), False)
     pass_again(7)
@@ -392,11 +404,10 @@
     spread[1][1]()
     spread[3][0]()
     spread[2][1]()
-    spread[3][1]()
     for copy in send_c:
         copy.wait()
     for j in range(tiles):
-        spread[j][2]()
+        spread[j][-1]()
 
     feats = cols[...].reshape(N_PLANE * rows, 512).T
     lane = lax.rem(y, 2) * 64
@@ -458,16 +469,19 @@
     brows = bank.shape[0]
     vmem = pl.BlockSpec(memory_space=pltpu.VMEM)
     hbm = pl.BlockSpec(memory_space=pl.ANY)
-    n_sems = 5 + 4 * CHUNKS + 15 + 4 * 30 + 1 + 4 * 12 + 4 * 38 + 10 + 7 + 15
+    n_sems = 5 + 4 * CHUNKS + 15 + 4 * 30 + 1 + 4 * 12 + 3 * 38 + 30 + 10 + 7 + 15
     gradient, factor = pl.pallas_call(
         kernel,
         out_shape=(
             jax.ShapeDtypeStruct((depth // 128, width), F32),
             jax.ShapeDtypeStruct((1, 128), F32),
         ),
-        in_specs=[vmem, vmem, vmem, hbm, hbm],
+        in_specs=[hbm] * 5,
         out_specs=(vmem, vmem),
         scratch_shapes=[
+            pltpu.VMEM((rows, depth), BF16),
+            pltpu.VMEM((rows, depth), BF16),
+            pltpu.VMEM((rows, depth), BF16),
             pltpu.VMEM((2, rows, depth // 2), BF16),
             pltpu.VMEM((2 * rows, depth // 2), BF16),
             pltpu.VMEM((2, depth // 4, width), BF16),
@@ -495,7 +509,7 @@
             pltpu.VMEM((7, 8, 128), F32),
             pltpu.VMEM((8, 128), F32),
             pltpu.VMEM((15, 8, 128), F32),
-            pltpu.SemaphoreType.DMA((5,)),
+            pltpu.SemaphoreType.DMA((8,)),
             pltpu.SemaphoreType.DMA((n_sems,)),
             pltpu.SemaphoreType.DMA((n_sems,)),
         ],

time: 111 us -> 108 us (0.973)
  Pallas kernels: 109 us -> 105 us
    pallas_call x1, Pallas kernels: 109 us -> 105 us  [local(): pl.pallas_call(kernel, out_shape=(jax.ShapeDtypeStruct((depth // 128, wid...]
where the time goes in v5:
time: 108 us; the launch traced here: 107 us
  Pallas kernels  105 us (97%)
  other arithmetic  2.25 us (2%)
    pallas_call x1, Pallas kernels, local(): pl.pallas_call(kernel, out_shape=(jax.ShapeDtypeStruct((depth // 128, wid...  105 us
    mul x1, other arithmetic, local(): return gradient * factor[0, 0]  2.25 us

profile of v5, /device:TPU:1, one launch (start us, length us, event | category | flops | bytes accessed | tf_op | source)
XLA Modules:
  0.0 107.5 jit_solution(7409997350078004295)
XLA Ops:
  0.0 105.2 %mmd_step.1 = (f32[32,1024]{1,0:T(8,128)}, f32[1,128]{1,0:T(1,128)}) custom-call(bf16[64,4096]{1,0:T(8,128)(2,1)} %lat_hbm.1, bf16[64,4096]{1,0:T(8,128)(2,1)} %shift_hbm.1, bf16[64,4096]{1,0:T(8,128)(2,1)} %scale_hbm.1, bf16[1024,1024]{1,0:T(8,128)(2,1)} %hw_hbm.1, bf16[2048,1024]{1,0:T(8,128)(2,1)} %bank_hbm.1), custom_call_target="tpu_custom_call" | custom-call | tf_op jit(solution)/shard_map/mmd_step/pallas_call | solution.py:473
  105.2 2.3 %broadcast_multiply_fusion = f32[32,1024]{1,0:T(8,128)} fusion(f32[32,1024]{1,0:T(8,128)} %get-tuple-element.7, f32[]{:T(128)} %bitcast.2), kind=kLoop, calls=%fused_computation | loop fusion | flops 32768 | bytes 262148 | tf_op jit(solution)/shard_map/mul | solution.py:521

commit v6 on v5

--- a/solution.py
+++ b/solution.py
@@ -64,12 +64,13 @@
     cut = {"xl": 1 - xl, "xh": 1 - xh}
     far_mate = {"xh": 1 - xh}
 
-    load_f = [
-        pltpu.make_async_copy(src, dst, loc.at[5 + n])
-        for n, (src, dst) in enumerate(((lat_hbm, lat), (shift_hbm, shift), (scale_hbm, scale)))
-    ]
-    for copy in load_f:
-        copy.start()
+    parts = rows // 16
+    load_f = []
+    for i in range(parts):
+        for n, (src, dst) in enumerate(((lat_hbm, lat), (shift_hbm, shift), (scale_hbm, scale))):
+            r = pl.ds(i * 16, 16)
+            load_f.append(pltpu.make_async_copy(src.at[r], dst.at[r], loc.at[5 + i * 3 + n]))
+            load_f[-1].start()
     barrier = pltpu.get_barrier_semaphore()
     for k in range(1, N_PLANE):
         pl.semaphore_signal(barrier, inc=1, device_id=on_plane(k)[0], device_id_type=MESH)
@@ -88,18 +89,47 @@
     for k in range(1, 4):
         load_b[k].start()
 
-    def modulate(i, _):
-        r = pl.ds(pl.multiple_of(i * 16, 16), 16)
+    for i in range(parts):
+        for n in range(3):
+            load_f[i * 3 + n].wait()
+        r = slice(i * 16, i * 16 + 16)
         f = lat[r, :].astype(F32)
         inverse = lax.rsqrt(jnp.mean(f * f, axis=1, keepdims=True) + 1e-06)
         h = (f * inverse * (1.0 + scale[r, :].astype(F32)) + shift[r, :].astype(F32)).astype(BF16)
         hid[0, r, :] = h[:, :half]
         hid[1, r, :] = h[:, half:]
-        return 0
-
-    for copy in load_f:
-        copy.wait()
-    lax.fori_loop(0, rows // 16, modulate, 0)
+    pl.semaphore_wait(barrier, N_PLANE - 1 + 7)
+
+    upper, lower = pl.ds(0, hrows), pl.ds(hrows, hrows)
+    send_h = [
+        send(hid.at[1 - xl, upper], lhs.at[pl.ds(rows, hrows)], pair),
+        send(hid.at[1 - xl, lower], lhs.at[pl.ds(rows + hrows, hrows)], cut),
+    ]
+    def unit_rows(q, lo, hi):
+        def step(i, _):
+            r = pl.ds(pl.multiple_of(i * 64, 64), 64)
+            b = bu[0, q, r, :].astype(F32)
+            bu[0, q, r, :] = (b * lax.rsqrt(jnp.sum(b * b, axis=1, keepdims=True) + 1e-06)).astype(BF16)
+            return 0
+
+        lax.fori_loop(lo, hi, step, 0)
+
+    load_b[0].wait()
+    own_q = xl * 2 + c
+    pair_q = (1 - xl) * 2 + c
+    per = quarter // CHUNKS
+    unit_rows(gone, 0, 1)
+
+    def piece(i):
+        return pl.ds(i * per, per)
+
+    send_b = [remote(bu.at[0, gone, piece(i)], bu.at[1, gone, piece(i)], cut) for i in range(CHUNKS)]
+    pass_core = [remote(bu.at[1, own_q, piece(i)], bu.at[1, own_q, piece(i)], core) for i in range(CHUNKS)]
+    pass_pair = [remote(bu.at[1, own_q, piece(i)], bu.at[1, own_q, piece(i)], pair) for i in range(CHUNKS)]
+    pass_last = [remote(bu.at[1, pair_q, piece(i)], bu.at[1, pair_q, piece(i)], core) for i in range(CHUNKS)]
+    send_b[0].start()
+    load_w.wait()
+    send_w = send(w.at[c], w.at[c], core)
     for p in range(N_PLANE // 2):
         for g in range(4):
             o = (g % 2) * strip + p * 128
@@ -111,45 +141,14 @@
         cols[j, me] = hs[me // 2, j]
     lhs[:rows] = hid[xl]
 
-    def unit_rows(q):
-        def step(i, _):
-            r = pl.ds(pl.multiple_of(i * 64, 64), 64)
-            b = bu[0, q, r, :].astype(F32)
-            bu[0, q, r, :] = (b * lax.rsqrt(jnp.sum(b * b, axis=1, keepdims=True) + 1e-06)).astype(BF16)
-            return 0
-
-        lax.fori_loop(0, quarter // 64, step, 0)
-
-    load_b[0].wait()
-    own_q = xl * 2 + c
-    pair_q = (1 - xl) * 2 + c
-    per = quarter // CHUNKS
-    unit_rows(gone)
-    pl.semaphore_wait(barrier, N_PLANE - 1 + 7)
-
-    upper, lower = pl.ds(0, hrows), pl.ds(hrows, hrows)
-    send_h = [
-        send(hid.at[1 - xl, upper], lhs.at[pl.ds(rows, hrows)], pair),
-        send(hid.at[1 - xl, lower], lhs.at[pl.ds(rows + hrows, hrows)], cut),
-    ]
-    load_w.wait()
-    send_w = send(w.at[c], w.at[c], core)
-
-    def piece(i):
-        return pl.ds(i * per, per)
-
-    send_b = [remote(bu.at[0, gone, piece(i)], bu.at[1, gone, piece(i)], cut) for i in range(CHUNKS)]
-    pass_core = [remote(bu.at[1, own_q, piece(i)], bu.at[1, own_q, piece(i)], core) for i in range(CHUNKS)]
-    pass_pair = [remote(bu.at[1, own_q, piece(i)], bu.at[1, own_q, piece(i)], pair) for i in range(CHUNKS)]
-    pass_last = [remote(bu.at[1, pair_q, piece(i)], bu.at[1, pair_q, piece(i)], core) for i in range(CHUNKS)]
-    send_b[0].start()
     send_c = []
     for k in NEAREST:
         device, m = on_plane(k)
         send_c.append(send(hs.at[m // 2], cols.at[:, me], device))
+    unit_rows(gone, 1, quarter // 64)
     for k in range(1, 4):
         load_b[k].wait()
-        unit_rows(lax.rem(gone + k, 4))
+        unit_rows(lax.rem(gone + k, 4), 0, quarter // 64)
 
     send_w.wait()
     for copy in send_h:
@@ -273,7 +272,7 @@
 
     batch = 2 * tiles * tile
 
-    def finish(j):
+    def near(j):
         u = units[j].reshape(tile, width)
         t = pairt[...]
         scores = lax.dot_general(u, t, (((1,), (1,)), ((), ())), preferred_element_type=F32)
@@ -282,8 +281,11 @@
         same = jnp.logical_and(row == column, jnp.logical_and(column >= 0, column < trows))
         weight = jnp.where(same, F32(0.0), jnp.exp(KERNEL_SCALE * scores)).astype(BF16)
         total = jnp.dot(weight, t, preferred_element_type=F32)
-        proof = total * (1.0 / (batch - 1)) - acc[j].reshape(tile, width) * (1.0 / (brows * 32))
-        proof = proof.reshape(4, 4, trows, width)
+        less = total * (brows * 32 / (batch - 1))
+        acc[j] = acc[j] - less.reshape(4, 4, trows, width)
+
+    def finish(j):
+        proof = acc[j] * (-1.0 / (brows * 32))
         acc[j] = proof
         wide[j] = proof.astype(BF16)
         sends = {}
@@ -378,9 +380,11 @@
     pass_again(7)
     weigh(1, 2, (core_q,), False)
     weigh(1, 3, (core_q,), False)
+    send_m.wait()
+    for j in range(tiles):
+        near(j)
     for i in range(CHUNKS):
         pass_last[i].wait()
-    send_m.wait()
     weigh(1, 0, late_q, False)
     send_p = [finish(0)]
     weigh(1, 1, late_q, False)
@@ -509,7 +513,7 @@
             pltpu.VMEM((7, 8, 128), F32),
             pltpu.VMEM((8, 128), F32),
             pltpu.VMEM((15, 8, 128), F32),
-            pltpu.SemaphoreType.DMA((8,)),
+            pltpu.SemaphoreType.DMA((17,)),
             pltpu.SemaphoreType.DMA((n_sems,)),
             pltpu.SemaphoreType.DMA((n_sems,)),
         ],

time: 108 us -> 108 us (level)
  no operation moved by 1% of the time
where the time goes in v6:
time: 108 us
  Pallas kernels  106 us (98%)
  other arithmetic  2.25 us (2%)
    pallas_call x1, Pallas kernels, local(): pl.pallas_call(kernel, out_shape=(jax.ShapeDtypeStruct((depth // 128, wid...  106 us
    mul x1, other arithmetic, local(): return gradient * factor[0, 0]  2.25 us

profile of v6, /device:TPU:1, one launch (start us, length us, event | category | flops | bytes accessed | tf_op | source)
XLA Modules:
  0.0 108.3 jit_solution(10352971783723651151)
XLA Ops:
  0.0 106.0 %mmd_step.1 = (f32[32,1024]{1,0:T(8,128)}, f32[1,128]{1,0:T(1,128)}) custom-call(bf16[64,4096]{1,0:T(8,128)(2,1)} %lat_hbm.1, bf16[64,4096]{1,0:T(8,128)(2,1)} %shift_hbm.1, bf16[64,4096]{1,0:T(8,128)(2,1)} %scale_hbm.1, bf16[1024,1024]{1,0:T(8,128)(2,1)} %hw_hbm.1, bf16[2048,1024]{1,0:T(8,128)(2,1)} %bank_hbm.1), custom_call_target="tpu_custom_call" | custom-call | tf_op jit(solution)/shard_map/mmd_step/pallas_call | solution.py:477
  106.0 2.3 %broadcast_multiply_fusion = f32[32,1024]{1,0:T(8,128)} fusion(f32[32,1024]{1,0:T(8,128)} %get-tuple-element.7, f32[]{:T(128)} %bitcast.2), kind=kLoop, calls=%fused_computation | loop fusion | flops 32768 | bytes 262148 | tf_op jit(solution)/shard_map/mul | solution.py:525
